TPU v7x, 32 devices: a whole 2x2x4 slice. The times are simulated.
32 devices in a mesh: tx: 4 (over z), ty: 4 (over y, core), gz: 2 (over x).
Axes of the slice: x: 2, y: 2, z: 4, core: 2. Of those that a mesh axis runs over, the one named last changes fastest.
Arguments:
- design: float32 [128, 1024, 256], P('tx', 'ty', 'gz'), may hold values from 0.05 to 0.95
- forward_edges: float32 [2, 12, 65536], P(None, None, ('tx', 'ty', 'gz')), may hold values from -6 to 6
- adjoint_edges: float32 [2, 12, 65536], P(None, None, ('tx', 'ty', 'gz')), may hold values from -6 to 6
- edge_basis: float32 [24, 12], replicated, may hold values from -1.75 to 1.75
- quad_weights: float32 [8], replicated, may hold values from 0.05 to 0.25
- slot_weights: bfloat16 [512, 16, 128], P(('tx', 'ty', 'gz')), may hold values from 0.049804688 to 1
- slot_elements: int32 [512, 16], P(('tx', 'ty', 'gz')), may hold values from 0 to 2047
- slot_blocks: int32 [512, 16], P(('tx', 'ty', 'gz')), may hold values from 0 to 8191
- slot_counts: int32 [32, 16], P(('tx', 'ty', 'gz')), may hold values from 1 to 16, 128 in all within a row
Outputs:
- projected: float32 [128, 1024, 256], P('tx', 'ty', 'gz')
- element_density: float32 [65536], P(('tx', 'ty', 'gz'))
Inputs may be any that keep to these rules, and one draw needn't show every extreme that they name: `slot_counts`: in every row of each partition the counts sum to 16 * 16 // 2 and the largest equals 16.
All inputs are finite; a program needn't handle non-finite values.
Results may differ from a plain program's by a relative error of at most 0.00055.
Values may be sent and summed in bfloat16 or wider, within the bound.
No kernel may reach another device: no remote copies, remote signals or barrier semaphores. Data moves between devices by JAX's collectives and lax.ppermute only.
A program may use at most 128 MiB of HBM per device.

v0:
```python
import functools
import math

import jax
import jax.numpy as jnp
from jax import lax
from jax.experimental import pallas as pl
from jax.experimental.pallas import tpu as pltpu
from jax.sharding import PartitionSpec as P


RADIUS = 8
LANES = 128
TAPS = RADIUS + 1
F32 = jnp.float32
BF16 = jnp.bfloat16
SMEM = pltpu.SMEM
VMEM = pltpu.VMEM
NT = ((1,), (1,))
TN = ((0,), (0,))


def iota(shape, dim):
    return lax.broadcasted_iota(jnp.int32, shape, dim)


def onehot(mask):
    return mask.astype(F32).astype(BF16)


def cone(distance):
    return jnp.maximum(TAPS - jnp.abs(distance), 0).astype(F32).astype(BF16)


def halves(x):
    high = x.astype(BF16)
    return high, (x - high.astype(F32)).astype(BF16)


def dot(a, b, contract=((1,), (0,)), precision=None):
    return lax.dot_general(
        a, b, (contract, ((), ())), preferred_element_type=F32, precision=precision
    )


def picker(first):
    return onehot(iota((RADIUS, LANES), 1) == iota((RADIUS, LANES), 0) + first)


def running(planes, length):
    add = lambda a, b: a + b
    box = [functools.reduce(add, planes[:TAPS])]
    for k in range(length + RADIUS - 1):
        box.append(box[-1] + (planes[k + TAPS] - planes[k]))
    total = functools.reduce(add, box[:TAPS])
    out = [total]
    for i in range(length - 1):
        total = total + (box[i + TAPS] - box[i])
        out.append(total)
    return out


def clipped(x):
    return jnp.clip(x, -0.5, 0.5)


def pack_kernel(
    n_ty, counts_ref, quad_ref, zoff_ref, basis_hbm, forward_hbm, adjoint_hbm, weights_hbm,
    elements_hbm, blocks_hbm, design_ref, pay_ref, up_edge_ref, down_edge_ref, basis_ref,
    forward_ref, adjoint_ref, weights_ref, elements_ref, blocks_ref, strip_ref, code_ref, sem,
):
    sources = (forward_hbm, adjoint_hbm, basis_hbm, elements_hbm, blocks_hbm, weights_hbm)
    targets = (forward_ref, adjoint_ref, basis_ref, elements_ref, blocks_ref, weights_ref)
    loads = [
        pltpu.make_async_copy(source, target, sem.at[2 + i])
        for i, (source, target) in enumerate(zip(sources, targets))
    ]
    for load in loads:
        load.start()
    cells_x, cells_y, _ = design_ref.shape
    tiles, capacity = elements_ref.shape
    points = quad_ref.shape[0]
    highest = lax.Precision.HIGHEST
    copies = [
        pltpu.make_async_copy(
            design_ref.at[pl.ds(start, RADIUS)], strip_ref.at[pl.ds(side * RADIUS, RADIUS)],
            sem.at[side],
        )
        for side, start in enumerate((0, cells_x - RADIUS))
    ]
    for copy in copies:
        copy.start()
    for load in loads:
        load.wait()

    terms, edges = 2 * forward_ref.shape[0], forward_ref.shape[0]
    point = iota((1, 3 * points), 1) % points
    quad = jnp.zeros((1, 3 * points), F32)
    for q in range(points):
        quad = quad + jnp.where(point == q, quad_ref[q], 0.0)
    twice = (iota((terms, edges), 0) // 2 == iota((terms, edges), 1)).astype(F32)
    basis = dot(twice, basis_ref[...], precision=highest)
    gram = dot(basis * quad, basis, NT, precision=highest)
    row, column = iota((terms, terms), 0), iota((terms, terms), 1)
    gram = jnp.where(row % 2 == 0, gram, -gram)
    gram = jnp.where(row % 2 == column % 2, gram, 0.0)
    adjoint = jnp.concatenate([adjoint_ref[k] for k in range(edges)], axis=0)
    forward = jnp.concatenate([forward_ref[k] for k in range(edges)], axis=0)
    sens = jnp.sum(forward * dot(gram, adjoint, precision=highest), axis=0, keepdims=True)
    groups = sens.shape[1] // LANES
    sens = jnp.concatenate([sens[:, g * LANES : (g + 1) * LANES] for g in range(groups)], axis=0)
    first, _ = halves(sens)
    second, third = halves(sens - first.astype(F32))
    parts = jnp.concatenate([first, second, third], axis=0)

    element, block = elements_ref[...], blocks_ref[...]
    codes = [
        element // LANES,
        element % LANES,
        block // cells_y + RADIUS,
        block % cells_y,
    ]
    place = iota((capacity, LANES), 1) - iota((capacity, LANES), 0)
    for index, code in enumerate(codes):
        code = code.astype(F32).astype(BF16)
        total = jnp.zeros((tiles, LANES), F32)
        for order, d in enumerate((0, -1, 1)):
            moved = dot(code, onehot(place == order * capacity))
            shift = (d * n_ty) % tiles
            if shift:
                moved = jnp.concatenate([moved[shift:], moved[:shift]], axis=0)
            if index == 2 and d:
                group = iota((tiles, LANES), 1) // capacity
                moved = moved + jnp.where(group == order, float(d * cells_x), 0.0)
            total = total + moved
        code_ref[index] = total

    @pl.loop(0, tiles, unroll=min(tiles, 16))
    def _(t):
        high, low, plane, line = (code_ref[index, pl.ds(t, 1), :] for index in range(4))
        lane = iota((1, LANES), 1)
        live = jnp.zeros((1, LANES), jnp.bool_)
        sources = []
        for order, d in enumerate((0, -1, 1)):
            source = lax.rem(t + (d * n_ty) % tiles, tiles)
            sources.append(source)
            at = lane - order * capacity
            live = live | ((at >= 0) & (at < capacity) & (at < counts_ref[0, source]))
        hit = onehot(iota((LANES, LANES), 0).astype(F32) == low)
        found = dot(parts, hit)
        found = (found[:groups] + found[groups : 2 * groups]) + found[2 * groups :]
        mine = iota((groups, LANES), 0).astype(F32) == high
        value = jnp.sum(jnp.where(mine, found, 0.0), axis=0, keepdims=True)
        value = jnp.where(live, value, 0.0).astype(BF16).astype(F32) * -0.5
        kind = iota((8, LANES), 0)
        meta = jnp.where(kind == 0, plane, jnp.where(kind == 1, line, value))
        meta = jnp.where(kind < 3, meta, 0.0)
        for order, source in enumerate(sources):
            pay_ref[t, order * capacity : (order + 1) * capacity, :] = weights_ref[source]
        pay_ref[t, 3 * capacity :, :] = meta.astype(BF16)

    pick = picker(zoff_ref[0])
    for side, edge_ref in enumerate((down_edge_ref, up_edge_ref)):
        copies[side].wait()

        @pl.loop(0, RADIUS, unroll=4)
        def _(p):
            plane = strip_ref[side * RADIUS + p] - 0.5
            edge_ref[p, :RADIUS] = plane[:RADIUS].astype(BF16)
            edge_ref[p, RADIUS : 2 * RADIUS] = plane[cells_y - RADIUS :].astype(BF16)
            flipped = dot(pick, plane.astype(BF16), NT).astype(BF16)
            for k in range(cells_y // LANES):
                start = (2 + k) * RADIUS
                edge_ref[p, start : start + RADIUS] = flipped[:, k * LANES : (k + 1) * LANES]


def main_kernel(design_ref, token_ref, up_ref, down_ref, strip_ref, sem):
    cells_x, cells_y, _ = design_ref.shape
    copies = [
        pltpu.make_async_copy(
            design_ref.at[pl.ds(start, RADIUS)], strip_ref.at[pl.ds(side * RADIUS, RADIUS)],
            sem.at[side],
        )
        for side, start in enumerate((0, cells_x - RADIUS))
    ]
    for copy in copies:
        copy.start()
    for side, main_ref in enumerate((down_ref, up_ref)):
        copies[side].wait()

        @pl.loop(0, RADIUS, unroll=2)
        def _(p):
            plane = strip_ref[side * RADIUS + p, RADIUS : cells_y - RADIUS, :]
            main_ref[p] = (plane - 0.5).astype(BF16)


def deposit_kernel(
    cells_y, slots, zoff_ref, design_ref, low_ref, high_ref, pay_ref, grid_ref, rows_out_ref,
    rim_ref, own_ref, flip_ref, weight_ref, code_ref, value_ref, code_smem, value_smem, sem,
):
    cells_x = design_ref.shape[0] // cells_y
    partners = pay_ref.shape[0]
    rim = RADIUS * cells_y
    own = cells_x * cells_y
    copy = pltpu.make_async_copy(design_ref, grid_ref.at[pl.ds(rim, own)], sem.at[0])
    copy.start()

    lane = iota((1, LANES), 1)
    upper = onehot(iota((LANES, LANES), 0) <= iota((LANES, LANES), 1))

    @pl.loop(0, partners, unroll=min(partners, 16))
    def _(p):
        weight_ref[pl.ds(pl.multiple_of(p * slots, 16), slots), :] = pay_ref[p, :slots, :].astype(F32)
        meta = pay_ref[p, slots : slots + 8, :].astype(F32)
        plane, line, value = meta[0:1], meta[1:2], meta[2:3]
        own_ref[pl.ds(p, 1), :] = ((plane - float(RADIUS)) * float(cells_y) + line).astype(jnp.int32)
        used = (plane >= 0.0) & (plane < float(cells_x + 2 * RADIUS)) & (value != 0.0)
        used = jnp.where(used & (lane < slots), 1.0, 0.0)
        order = dot(jnp.broadcast_to(used, (8, LANES)).astype(BF16), upper)[:1]
        place = jnp.where(used > 0.0, order - 1.0, -1.0)
        hit = onehot(iota((LANES, LANES), 0).astype(F32) == place)
        kind = iota((8, LANES), 0)
        meta = jnp.where(kind == 3, lane.astype(F32), jnp.where(kind < 3, meta, 0.0))
        moved = dot(meta.astype(BF16), hit, NT)
        code = (moved[0:1] * float(cells_y) + moved[1:2]) * float(LANES) + moved[3:4]
        code = jnp.where(lane == LANES - 1, order[:, LANES - 1 :], code)
        code_ref[pl.ds(p, 1), :] = code.astype(jnp.int32)
        value_ref[pl.ds(p, 1), :] = moved[2:3]

    lists = [
        pltpu.make_async_copy(code_ref, code_smem, sem.at[1]),
        pltpu.make_async_copy(value_ref, value_smem, sem.at[2]),
    ]
    for move in lists:
        move.start()
    zeros = jnp.zeros((cells_y, LANES), F32)
    for p in range(RADIUS):
        grid_ref[p * cells_y : (p + 1) * cells_y, :] = zeros
        grid_ref[rim + own + p * cells_y : rim + own + (p + 1) * cells_y, :] = zeros
    for move in lists:
        move.wait()
    copy.wait()

    @pl.loop(0, partners)
    def _(p):
        @pl.loop(0, (code_smem[p, LANES - 1] + 3) // 4)
        def _(j):
            for k in range(4):
                code = code_smem[p, j * 4 + k]
                row = code // LANES
                amount = value_smem[p, j * 4 + k] * weight_ref[pl.ds(p * slots + code % LANES, 1), :]
                grid_ref[pl.ds(row, 1), :] = grid_ref[pl.ds(row, 1), :] + amount

    total = cells_x + 2 * RADIUS
    pick = picker(zoff_ref[0])

    @pl.loop(0, cells_x, unroll=4)
    def _(x):
        plane = clipped(grid_ref[pl.ds(rim + x * cells_y, cells_y), :] - 0.5)
        flip_ref[x + RADIUS] = dot(pick, plane.astype(BF16), NT)

    for source_ref, base in ((low_ref, 0), (high_ref, RADIUS + cells_x)):
        @pl.loop(0, RADIUS, unroll=4)
        def _(p):
            plane = grid_ref[pl.ds((base + p) * cells_y, cells_y), :]
            deposited = dot(pick, plane.astype(BF16), NT)
            raw = jnp.concatenate(
                [
                    source_ref[p, (2 + k) * RADIUS : (3 + k) * RADIUS].astype(F32)
                    for k in range(cells_y // LANES)
                ],
                axis=1,
            )
            flip_ref[base + p] = clipped(raw + deposited)

    for source_ref, base in ((low_ref, 0), (high_ref, RADIUS + cells_x)):
        for p in range(RADIUS):
            for k, start in enumerate((0, cells_y - RADIUS)):
                at = (base + p) * cells_y + start
                edge = source_ref[p, k * RADIUS : (k + 1) * RADIUS].astype(F32)
                grid_ref[at : at + RADIUS, :] = grid_ref[at : at + RADIUS, :] + edge

    for k, start in enumerate((0, cells_y - RADIUS)):
        planes = []
        for e in range(total):
            at = e * cells_y + start
            bias = 0.5 if RADIUS <= e < RADIUS + cells_x else 0.0
            planes.append(clipped(grid_ref[at : at + RADIUS, :] - bias))
        for i, value in enumerate(running(planes, cells_x)):
            rows_out_ref[i, k * RADIUS : (k + 1) * RADIUS, :] = value

    for i, value in enumerate(running([flip_ref[e] for e in range(total)], cells_x)):
        rim_ref[i] = value.astype(BF16)


def edge_kernel(zoff_ref, rows_ref, rim_ref, first_ref, last_ref):
    cells_x, double, cells_z = rows_ref.shape
    cells_y = rim_ref.shape[2]
    weights = cone(iota((cells_z, cells_z), 0) - iota((cells_z, cells_z), 1))
    weights = jnp.concatenate([weights, weights], axis=0)
    side = cone(iota((RADIUS, cells_z), 0) + zoff_ref[1] - iota((RADIUS, cells_z), 1))
    rows = rows_ref[...].reshape(cells_x * double, cells_z)
    value = dot(jnp.concatenate(halves(rows), axis=1), weights)
    for x in range(cells_x):
        for k, out_ref in enumerate((first_ref, last_ref)):
            start = 0 if k == 0 else cells_y - LANES
            shift = 0 if k == 0 else LANES - RADIUS
            rim = rim_ref[x, :, start : start + LANES][:, shift : shift + RADIUS]
            at = x * double + k * RADIUS
            out_ref[x] = (value[at : at + RADIUS] + dot(rim, side, TN)).astype(BF16)


def finish_kernel(
    scale_total, zoff_ref, own_ref, grid_ref, low_ref, high_ref, rim_ref, before_ref, after_ref,
    pay_ref, out_ref, ratio_ref, rims_ref, smooth_ref, proj_ref, picked_ref, rows_ref, sem, own_sem,
):
    cells_x, _, cells_y = rim_ref.shape
    cells_z = out_ref.shape[1]
    partners = pay_ref.shape[0]
    capacity = picked_ref.shape[0] // partners
    total = cells_x + 2 * RADIUS
    inner = cells_y - 2 * RADIUS
    chunk = 16
    fetch = pltpu.make_async_copy(own_ref, rows_ref, own_sem)
    fetch.start()

    for source_ref, base, into in ((low_ref, 0, 0), (high_ref, RADIUS + cells_x, RADIUS)):
        @pl.loop(0, RADIUS)
        def _(p):
            at = pl.multiple_of((base + p) * cells_y, 8)
            to = pl.multiple_of((into + p) * cells_y, 8)
            main = grid_ref[pl.ds(at + RADIUS, inner), :] + source_ref[p].astype(F32)
            rims_ref[pl.ds(to + RADIUS, inner), :] = clipped(main)
            for start in (0, cells_y - RADIUS):
                value = grid_ref[pl.ds(at + start, RADIUS), :]
                rims_ref[pl.ds(to + start, RADIUS), :] = clipped(value)

    @pl.loop(0, cells_y // chunk)
    def _(j):
        planes = []
        start = pl.multiple_of(j * chunk, chunk)
        for e in range(total):
            if RADIUS <= e < RADIUS + cells_x:
                at = pl.multiple_of(e * cells_y + start, chunk)
                value = clipped(grid_ref[pl.ds(at, chunk), :] - 0.5)
            else:
                side = e if e < RADIUS else e - cells_x
                value = rims_ref[pl.ds(pl.multiple_of(side * cells_y + start, chunk), chunk), :]
            planes.append(value)
        for i, value in enumerate(running(planes, cells_x)):
            smooth_ref[i, pl.ds(start, chunk), :] = value.astype(BF16)

    across = cone(iota((cells_y, cells_y), 0) - iota((cells_y, cells_y), 1))
    along = cone(iota((cells_z, cells_z), 0) - iota((cells_z, cells_z), 1))
    along = jnp.concatenate([along, along], axis=0)
    side = cone(iota((RADIUS, cells_z), 0) + zoff_ref[1] - iota((RADIUS, cells_z), 1))
    column = iota((cells_y, 2 * RADIUS), 1)
    place = jnp.where(column < RADIUS, column - RADIUS, column - RADIUS + cells_y)
    edge = cone(place - iota((cells_y, 2 * RADIUS), 0))
    z = iota((1, cells_z), 1) + zoff_ref[2]
    inside = jnp.zeros((1, cells_z), F32)
    for offset in range(-RADIUS, RADIUS + 1):
        good = (z + offset >= 0) & (z + offset < zoff_ref[3])
        inside = inside + jnp.where(good, float(TAPS - abs(offset)), 0.0)
    scale = 8.0 / (scale_total * inside)
    top = math.tanh(4.0)
    step = 4

    def copy(g):
        rows = pl.ds(pl.multiple_of(g * step * cells_y, 8), step * cells_y)
        return pltpu.make_async_copy(proj_ref.at[rows], out_ref.at[rows], sem.at[g])

    @pl.loop(0, cells_x // step)
    def _(g):
        rims = rim_ref[pl.ds(g * step, step)].reshape(step * RADIUS, cells_y)
        rims = dot(rims, across).astype(BF16)
        for pair in range(step // 2):
            x = g * step + 2 * pair
            both = jnp.concatenate([smooth_ref[x], smooth_ref[x + 1]], axis=1)
            both = dot(across, both)
            for k in range(2):
                half = jnp.concatenate(halves(both[:, k * cells_z : (k + 1) * cells_z]), axis=1)
                value = dot(half, along)
                at = (2 * pair + k) * RADIUS
                value = value + dot(rims[at : at + RADIUS], side, TN)
                ends = jnp.concatenate(
                    [before_ref[x + k].astype(F32), after_ref[x + k].astype(F32)], axis=0
                ).astype(BF16)
                value = value + dot(edge, ends)
                value = (top + jnp.tanh(value * scale)) * (1.0 / (2.0 * top))
                proj_ref[pl.ds(pl.multiple_of((x + k) * cells_y, 8), cells_y), :] = value
        copy(g).start()

    fetch.wait()

    @pl.loop(0, partners)
    def _(p):
        for s in range(capacity):
            row = rows_ref[p, s]
            picked_ref[pl.ds(p * capacity + s, 1), :] = proj_ref[pl.ds(row, 1), :]

    ones = jnp.ones((8, cells_z), BF16)
    group = LANES // capacity

    @pl.loop(0, partners * capacity // LANES)
    def _(c):
        w = pay_ref[pl.ds(c * group, group), :capacity, :].reshape(LANES, cells_z)
        picked = picked_ref[pl.ds(pl.multiple_of(c * LANES, LANES), LANES), :]
        high, low = halves(w.astype(F32) * picked)
        amount = dot(ones, high, NT) + dot(ones, low, NT)
        ratio_ref[pl.ds(c, 1), :] = (amount / dot(ones, w, NT))[:1]

    @pl.loop(0, cells_x // step)
    def _(g):
        copy(g).wait()


def back_kernel(counts_ref, elements_ref, ratio_ref, out_ref):
    tiles, capacity = elements_ref.shape
    high_count = out_ref.shape[0]
    total = jnp.zeros(out_ref.shape, F32)
    for t in range(tiles):
        element = elements_ref[pl.ds(t, 1), :]
        live = iota((1, capacity), 1) < counts_ref[0, t]
        ratio = jnp.where(live, ratio_ref[pl.ds(t, 1), :], 0.0)
        lane = onehot(iota((LANES, capacity), 0) == (element & (LANES - 1)))
        spread = jnp.where(iota((high_count, capacity), 0) == element // LANES, ratio, 0.0)
        high, low = halves(spread)
        total = total + (dot(high, lane, NT) + dot(low, lane, NT))
    out_ref[...] = total


def update(
    design,
    forward_edges,
    adjoint_edges,
    edge_basis,
    quad_weights,
    slot_weights,
    slot_elements,
    slot_blocks,
    slot_counts,
):
    cells_x, cells_y, cells_z = design.shape
    tiles, capacity = slot_elements.shape
    n_tx, n_ty, n_gz = (lax.axis_size(a) for a in ("tx", "ty", "gz"))
    if cells_z != LANES or cells_y != 256 or n_gz != 2:
        raise NotImplementedError
    slots = 3 * capacity
    edge_count, elements = forward_edges.shape[1:]
    rows_ext = (cells_x + 2 * RADIUS) * cells_y
    gz = lax.axis_index("gz")
    zoff = jnp.stack(
        [
            jnp.where(gz == 0, cells_z - RADIUS, 0),
            jnp.where(gz == 0, cells_z, -RADIUS),
            gz * cells_z,
            jnp.int32(n_gz * cells_z),
        ]
    ).astype(jnp.int32)
    whole = pl.BlockSpec(memory_space=VMEM)
    scalars = pl.BlockSpec(memory_space=SMEM)
    anywhere = pl.BlockSpec(memory_space=pltpu.HBM)
    shape = jax.ShapeDtypeStruct
    params = lambda mib: pltpu.CompilerParams(vmem_limit_bytes=mib << 20)

    inner = cells_y - 2 * RADIUS
    edge_rows = 2 * RADIUS + RADIUS * cells_y // LANES
    payload, up_edge, down_edge = pl.pallas_call(
        functools.partial(pack_kernel, n_ty),
        out_shape=(
            shape((tiles, slots + 8, LANES), BF16),
            shape((RADIUS, edge_rows, LANES), BF16),
            shape((RADIUS, edge_rows, LANES), BF16),
        ),
        in_specs=[scalars] * 3 + [anywhere] * 7,
        out_specs=(whole,) * 3,
        scratch_shapes=[
            VMEM(edge_basis.shape[::-1], F32),
            VMEM((edge_count, 2, elements), F32),
            VMEM((edge_count, 2, elements), F32),
            VMEM(slot_weights.shape, BF16),
            VMEM(slot_elements.shape, jnp.int32),
            VMEM(slot_blocks.shape, jnp.int32),
            VMEM((2 * RADIUS, cells_y, cells_z), F32),
            VMEM((4, tiles, LANES), F32),
            pltpu.SemaphoreType.DMA((8,)),
        ],
        name="pack",
    )(
        slot_counts,
        quad_weights,
        zoff,
        edge_basis.T,
        forward_edges.transpose(1, 0, 2),
        adjoint_edges.transpose(1, 0, 2),
        slot_weights,
        slot_elements,
        slot_blocks,
        design,
    )

    arrived = lax.all_to_all(payload, ("tx", "ty"), split_axis=0, concat_axis=0, tiled=True)
    up = [(i, (i + 1) % n_tx) for i in range(n_tx)]
    down = [(t, s) for s, t in up]
    low_edge = lax.ppermute(up_edge, "tx", up)
    high_edge = lax.ppermute(down_edge, "tx", down)
    main = shape((RADIUS, inner, LANES), BF16)
    call = pl.pallas_call(
        main_kernel,
        out_shape=(main, main),
        in_specs=[anywhere, anywhere],
        out_specs=(whole, whole),
        scratch_shapes=[
            VMEM((2 * RADIUS, cells_y, cells_z), F32),
            pltpu.SemaphoreType.DMA((2,)),
        ],
        name="main_rims",
    )
    up_main, down_main = call(design, up_edge)
    low_main = lax.ppermute(up_main, "tx", up)
    high_main = lax.ppermute(down_main, "tx", down)

    grid, edge_smooth, rim, rows_own = pl.pallas_call(
        functools.partial(deposit_kernel, cells_y, slots),
        out_shape=(
            shape((rows_ext, cells_z), F32),
            shape((cells_x, 2 * RADIUS, cells_z), F32),
            shape((cells_x, RADIUS, cells_y), BF16),
            shape((tiles, LANES), jnp.int32),
        ),
        in_specs=[scalars, anywhere] + [whole] * 3,
        out_specs=(whole,) * 4,
        scratch_shapes=[
            VMEM((cells_x + 2 * RADIUS, RADIUS, cells_y), F32),
            VMEM((tiles * slots, LANES), F32),
            VMEM((tiles, LANES), jnp.int32),
            VMEM((tiles, LANES), F32),
            SMEM((tiles, LANES), jnp.int32),
            SMEM((tiles, LANES), F32),
            pltpu.SemaphoreType.DMA((3,)),
        ],
        compiler_params=params(16),
        name="deposit",
    )(zoff, design.reshape(cells_x * cells_y, cells_z), low_edge, high_edge, arrived)

    rim = lax.ppermute(rim, "gz", [(0, 1), (1, 0)])
    edge = shape((cells_x, RADIUS, cells_z), BF16)
    first, last = pl.pallas_call(
        edge_kernel,
        out_shape=(edge, edge),
        in_specs=[scalars, whole, whole],
        out_specs=(whole, whole),
        compiler_params=params(16),
        name="edges",
    )(zoff, edge_smooth, rim)
    up = [(i, (i + 1) % n_ty) for i in range(n_ty)]
    down = [(t, s) for s, t in up]
    before = lax.ppermute(last, "ty", up)
    after = lax.ppermute(first, "ty", down)

    projected, ratios = pl.pallas_call(
        functools.partial(finish_kernel, float(TAPS**4)),
        out_shape=(
            shape((cells_x * cells_y, cells_z), F32),
            shape((tiles * capacity // LANES, LANES), F32),
        ),
        in_specs=[scalars] + [whole] * 8,
        out_specs=(anywhere, whole),
        scratch_shapes=[
            VMEM((2 * RADIUS * cells_y, cells_z), F32),
            VMEM((cells_x, cells_y, cells_z), BF16),
            VMEM((cells_x * cells_y, cells_z), F32),
            VMEM((tiles * capacity, cells_z), F32),
            SMEM((tiles, LANES), jnp.int32),
            pltpu.SemaphoreType.DMA((cells_x // 4,)),
            pltpu.SemaphoreType.DMA,
        ],
        compiler_params=params(24),
        name="finish",
    )(zoff, rows_own, grid, low_main, high_main, rim, before, after, arrived)

    ratios = ratios.reshape(tiles, capacity)
    ratios = lax.all_to_all(ratios, ("tx", "ty"), split_axis=0, concat_axis=0, tiled=True)
    density = pl.pallas_call(
        back_kernel,
        out_shape=shape((elements // LANES, LANES), F32),
        in_specs=[scalars, whole, whole],
        out_specs=whole,
        compiler_params=params(16),
        name="to_elements",
    )(slot_counts, slot_elements, ratios)
    return projected.reshape(design.shape), density.reshape(elements)


def solution(mesh):
    in_specs = (
        P("tx", "ty", "gz"),
        P(None, None, ("tx", "ty", "gz")),
        P(None, None, ("tx", "ty", "gz")),
        P(),
        P(),
        P(("tx", "ty", "gz"), None, None),
        P(("tx", "ty", "gz"), None),
        P(("tx", "ty", "gz"), None),
        P(("tx", "ty", "gz"), None),
    )
    out_specs = (P("tx", "ty", "gz"), P(("tx", "ty", "gz")))
    return jax.shard_map(update, mesh=mesh, in_specs=in_specs, out_specs=out_specs, check_vma=False)
```

profile of v0, /device:TPU:0, one launch (start us, length us, event | category | flops | bytes accessed | tf_op | source)
XLA Modules:
  0.0 87.1 jit_solution(2698263580994702355)
XLA Ops:
  0.6 0.7 pad_add_fusion.zoff_ref
  1.3 0.0 copy-start.2
  1.3 4.3 %pack.1 = (bf16[16,56,128]{2,1,0:T(8,128)(2,1)}, bf16[8,32,128]{2,1,0:T(8,128)(2,1)}, bf16[8,32,128]{2,1,0:T(8,128)(2,1)}) custom-call(s32[1,16]{1,0:T(1,128)} %counts_ref.3, f32[8]{0:T(128)} %quad_ref.1, s32[4]{0:T(128)} %pad_add_fusion.zoff_ref, f32[12,24]{1,0:T(8,128)} %bitcast.16, f32[12,2,2048]{2,1,0:T(2,128)} %bitcast.13, f32[12,2,2048]{2,1,0:T(2,128)} %bitcast.14, ...), custom_call_target="tpu_custom_call" | custom-call | tf_op jit(solution)/shard_map/pack/pallas_call | solution.py:469
  5.6 0.0 copy-start.5
  5.6 0.0 copy-start.4
  5.6 7.6 %all-to-all-start = ((bf16[16,56,128]{2,1,0:T(8,128)(2,1)}), bf16[16,56,128]{2,1,0:T(8,128)(2,1)S(1)}, u32[]{:S(2)}, u32[]{:S(2)}) async-start(bf16[16,56,128]{2,1,0:T(8,128)(2,1)} %get-tuple-element.17), calls=%async_computation | async-start | bytes 458752 | tf_op jit(solution)/shard_map/all_to_all | solution.py:503
  13.2 2.6 %main_rims.1 = (bf16[8,240,128]{2,1,0:T(8,128)(2,1)}, bf16[8,240,128]{2,1,0:T(8,128)(2,1)}) custom-call(f32[32,256,128]{2,1,0:T(8,128)} %design_ref.3, bf16[8,32,128]{2,1,0:T(8,128)(2,1)} %get-tuple-element.15.token_ref), custom_call_target="tpu_custom_call" | custom-call | tf_op jit(solution)/shard_map/main_rims/pallas_call | solution.py:520
  15.7 2.0 %collective-permute-start.2 = (bf16[8,240,128]{2,1,0:T(8,128)(2,1)}, bf16[8,240,128]{2,1,0:T(8,128)(2,1)S(1)}, u32[]{:S(2)}, u32[]{:S(2)}) collective-permute-start(bf16[8,240,128]{2,1,0:T(8,128)(2,1)} %get-tuple-element.20), channel_id=1, source_target_pairs={{0,8},{8,16},{16,24},{24,0},{1,9},{9,17},{17,25},{25,1},{2,10},{10... | collective-permute-start | bytes 1474568 | tf_op jit(solution)/shard_map/ppermute | solution.py:521
  17.7 1.9 %collective-permute-start.3 = (bf16[8,240,128]{2,1,0:T(8,128)(2,1)}, bf16[8,240,128]{2,1,0:T(8,128)(2,1)S(1)}, u32[]{:S(2)}, u32[]{:S(2)}) collective-permute-start(bf16[8,240,128]{2,1,0:T(8,128)(2,1)} %get-tuple-element.21), channel_id=1, source_target_pairs={{8,0},{16,8},{24,16},{0,24},{9,1},{17,9},{25,17},{1,25},{10,2},{18... | collective-permute-start | bytes 1474568 | tf_op jit(solution)/shard_map/ppermute | solution.py:522
  19.6 0.0 copy-done.5
  19.6 1.9 %collective-permute-start.1 = (bf16[8,32,128]{2,1,0:T(8,128)(2,1)S(1)}, bf16[8,32,128]{2,1,0:T(8,128)(2,1)S(1)}, u32[]{:S(2)}, u32[]{:S(2)}) collective-permute-start(bf16[8,32,128]{2,1,0:T(8,128)(2,1)S(1)} %copy-done.5), channel_id=1, source_target_pairs={{8,0},{16,8},{24,16},{0,24},{9,1},{17,9},{25,17},{1,25},{10,2},{18... | collective-permute-start | bytes 196616 | tf_op jit(solution)/shard_map/ppermute | solution.py:507
  21.6 0.0 copy-done.4
  21.6 0.1 collective-permute-start
  21.7 21.8 %collective-permute-done.1.high_ref = bf16[8,32,128]{2,1,0:T(8,128)(2,1)S(1)} collective-permute-done((bf16[8,32,128]{2,1,0:T(8,128)(2,1)S(1)}, bf16[8,32,128]{2,1,0:T(8,128)(2,1)S(1)}, u32[]{:S(2)}, u32[]{:S(2)}) %collective-permute-start.1) | collective-permute-done | bytes 65568 | tf_op jit(solution)/shard_map/ppermute | solution.py:507
  43.4 2.3 %collective-permute-done.low_ref = bf16[8,32,128]{2,1,0:T(8,128)(2,1)S(1)} collective-permute-done((bf16[8,32,128]{2,1,0:T(8,128)(2,1)S(1)}, bf16[8,32,128]{2,1,0:T(8,128)(2,1)S(1)}, u32[]{:S(2)}, u32[]{:S(2)}) %collective-permute-start) | collective-permute-done | bytes 65568 | tf_op jit(solution)/shard_map/ppermute | solution.py:506
  45.7 0.0 all-to-all-done.pay_ref
  45.7 0.0 copy-done.2
  45.7 0.0 copy-start
  45.7 2.2 %copy-done = f32[32,256,128]{2,1,0:T(8,128)S(1)} copy-done((f32[32,256,128]{2,1,0:T(8,128)S(1)}, f32[32,256,128]{2,1,0:T(8,128)}, u32[]{:S(2)}) %copy-start) | copy-done | bytes 4194328
  47.9 7.9 %deposit.1 = (f32[12288,128]{1,0:T(8,128)S(1)}, f32[32,16,128]{2,1,0:T(8,128)S(1)}, bf16[32,8,256]{2,1,0:T(8,128)(2,1)S(1)}, s32[16,128]{1,0:T(8,128)S(1)}) custom-call(s32[4]{0:T(128)S(1)} %copy-done.2, f32[8192,128]{1,0:T(8,128)S(1)} %bitcast.11, bf16[8,32,128]{2,1,0:T(8,128)(2,1)S(1)} %collective-permute-done.low_ref, ...), custom_call_target="tpu_custom_call" | custom-call | tf_op jit(solution)/shard_map/deposit/pallas_call | solution.py:524
  55.9 0.0 copy-start.1
  55.9 0.0 copy-start.3
  55.9 1.5 %collective-permute-start.4 = (bf16[32,8,256]{2,1,0:T(8,128)(2,1)S(1)}, bf16[32,8,256]{2,1,0:T(8,128)(2,1)S(1)}, u32[]{:S(2)}, u32[]{:S(2)}) collective-permute-start(bf16[32,8,256]{2,1,0:T(8,128)(2,1)S(1)} %get-tuple-element.22), channel_id=1, source_target_pairs={{0,1},{1,0},{2,3},{3,2},{4,5},{5,4},{6,7},{7,6},{8,9},{9,8},{10,11... | collective-permute-start | bytes 393224 | tf_op jit(solution)/shard_map/ppermute | solution.py:547
  57.4 3.5 %collective-permute-done.4.rim_ref = bf16[32,8,256]{2,1,0:T(8,128)(2,1)S(1)} collective-permute-done((bf16[32,8,256]{2,1,0:T(8,128)(2,1)S(1)}, bf16[32,8,256]{2,1,0:T(8,128)(2,1)S(1)}, u32[]{:S(2)}, u32[]{:S(2)}) %collective-permute-start.4) | collective-permute-done | bytes 131104 | tf_op jit(solution)/shard_map/ppermute | solution.py:547
  60.9 1.2 %edges.1 = (bf16[32,8,128]{2,1,0:T(8,128)(2,1)S(1)}, bf16[32,8,128]{2,1,0:T(8,128)(2,1)S(1)}) custom-call(s32[4]{0:T(128)S(1)} %copy-done.2, f32[32,16,128]{2,1,0:T(8,128)S(1)} %get-tuple-element.23.rows_ref, bf16[32,8,256]{2,1,0:T(8,128)(2,1)S(1)} %collective-permute-done.4.rim_ref), custom_call_target="tpu_custom_call" | custom-call | tf_op jit(solution)/shard_map/edges/pallas_call | solution.py:549
  62.1 0.1 collective-permute-start.5
  62.2 1.7 %collective-permute-start.6 = (bf16[32,8,128]{2,1,0:T(8,128)(2,1)S(1)}, bf16[32,8,128]{2,1,0:T(8,128)(2,1)S(1)}, u32[]{:S(2)}, u32[]{:S(2)}) collective-permute-start(bf16[32,8,128]{2,1,0:T(8,128)(2,1)S(1)} %get-tuple-element.25), channel_id=1, source_target_pairs={{2,0},{4,2},{6,4},{0,6},{3,1},{5,3},{7,5},{1,7},{10,8},{12,10},{14... | collective-permute-start | bytes 196616 | tf_op jit(solution)/shard_map/ppermute | solution.py:560
  63.9 0.0 collective-permute-done.2.low_ref
  63.9 0.0 collective-permute-done.3.high_ref
  63.9 1.9 %collective-permute-done.5.before_ref = bf16[32,8,128]{2,1,0:T(8,128)(2,1)S(1)} collective-permute-done((bf16[32,8,128]{2,1,0:T(8,128)(2,1)S(1)}, bf16[32,8,128]{2,1,0:T(8,128)(2,1)S(1)}, u32[]{:S(2)}, u32[]{:S(2)}) %collective-permute-start.5) | collective-permute-done | bytes 65568 | tf_op jit(solution)/shard_map/ppermute | solution.py:559
  65.9 0.0 collective-permute-done.6.after_ref
  65.9 8.9 %finish.1 = (f32[8192,128]{1,0:T(8,128)}, f32[2,128]{1,0:T(2,128)S(1)}) custom-call(s32[4]{0:T(128)S(1)} %copy-done.2, s32[16,128]{1,0:T(8,128)S(1)} %get-tuple-element.18.own_ref, f32[12288,128]{1,0:T(8,128)S(1)} %get-tuple-element.19.grid_ref, bf16[8,240,128]{2,1,0:T(8,128)(2,1)S(1)} %collective-permute-done.2.low_ref, ...), custom_call_target="tpu_custom_call" | custom-call | tf_op jit(solution)/shard_map/finish/pallas_call | solution.py:562
  74.8 0.1 all_to_all.11
  74.9 10.4 %all_to_all.16 = f32[16,1,16]{2,1,0:T(1,128)S(1)} all-to-all(f32[16,1,16]{2,1,0:T(1,128)S(1)} %bitcast.15), channel_id=1, replica_groups=mesh['tx'=4,'ty'=4,'gz'=2] {'tx','ty'}, dimensions={0} | all-to-all | bytes 2048 | tf_op jit(solution)/shard_map/all_to_all | solution.py:584
  85.3 0.0 copy-done.1
  85.3 0.0 copy-done.3
  85.3 1.8 %to_elements.1 = f32[16,128]{1,0:T(8,128)} custom-call(s32[1,16]{1,0:T(1,128)S(1)} %copy-done.3, s32[16,16]{1,0:T(8,128)S(1)} %copy-done.1, f32[16,16]{1,0:T(8,128)S(1)} %bitcast.12), custom_call_target="tpu_custom_call" | custom-call | tf_op jit(solution)/shard_map/to_elements/pallas_call | solution.py:585
Async XLA Ops:
  1.3 44.4 %copy-start.2 = (s32[4]{0:T(128)S(1)}, s32[4]{0:T(128)}, u32[]{:S(2)}) copy-start(s32[4]{0:T(128)} %pad_add_fusion.zoff_ref) | copy-start | bytes 52
  5.6 14.0 %copy-start.5 = (bf16[8,32,128]{2,1,0:T(8,128)(2,1)S(1)}, bf16[8,32,128]{2,1,0:T(8,128)(2,1)}, u32[]{:S(2)}) copy-start(bf16[8,32,128]{2,1,0:T(8,128)(2,1)} %get-tuple-element.16) | copy-start | bytes 196612
  5.6 16.0 %copy-start.4 = (bf16[8,32,128]{2,1,0:T(8,128)(2,1)S(1)}, bf16[8,32,128]{2,1,0:T(8,128)(2,1)}, u32[]{:S(2)}) copy-start(bf16[8,32,128]{2,1,0:T(8,128)(2,1)} %get-tuple-element.15.token_ref) | copy-start | bytes 196612
  5.6 40.1 %all-to-all-start = ((bf16[16,56,128]{2,1,0:T(8,128)(2,1)}), bf16[16,56,128]{2,1,0:T(8,128)(2,1)S(1)}, u32[]{:S(2)}, u32[]{:S(2)}) async-start(bf16[16,56,128]{2,1,0:T(8,128)(2,1)} %get-tuple-element.17), calls=%async_computation | async-start | bytes 458752 | tf_op jit(solution)/shard_map/all_to_all | solution.py:503
  15.7 48.2 %collective-permute-start.2 = (bf16[8,240,128]{2,1,0:T(8,128)(2,1)}, bf16[8,240,128]{2,1,0:T(8,128)(2,1)S(1)}, u32[]{:S(2)}, u32[]{:S(2)}) collective-permute-start(bf16[8,240,128]{2,1,0:T(8,128)(2,1)} %get-tuple-element.20), channel_id=1, source_target_pairs={{0,8},{8,16},{16,24},{24,0},{1,9},{9,17},{17,25},{25,1},{2,10},{10... | collective-permute-start | bytes 1474568 | tf_op jit(solution)/shard_map/ppermute | solution.py:521
  17.7 46.2 %collective-permute-start.3 = (bf16[8,240,128]{2,1,0:T(8,128)(2,1)}, bf16[8,240,128]{2,1,0:T(8,128)(2,1)S(1)}, u32[]{:S(2)}, u32[]{:S(2)}) collective-permute-start(bf16[8,240,128]{2,1,0:T(8,128)(2,1)} %get-tuple-element.21), channel_id=1, source_target_pairs={{8,0},{16,8},{24,16},{0,24},{9,1},{17,9},{25,17},{1,25},{10,2},{18... | collective-permute-start | bytes 1474568 | tf_op jit(solution)/shard_map/ppermute | solution.py:522
  19.6 23.8 %collective-permute-start.1 = (bf16[8,32,128]{2,1,0:T(8,128)(2,1)S(1)}, bf16[8,32,128]{2,1,0:T(8,128)(2,1)S(1)}, u32[]{:S(2)}, u32[]{:S(2)}) collective-permute-start(bf16[8,32,128]{2,1,0:T(8,128)(2,1)S(1)} %copy-done.5), channel_id=1, source_target_pairs={{8,0},{16,8},{24,16},{0,24},{9,1},{17,9},{25,17},{1,25},{10,2},{18... | collective-permute-start | bytes 196616 | tf_op jit(solution)/shard_map/ppermute | solution.py:507
  21.6 24.2 %collective-permute-start = (bf16[8,32,128]{2,1,0:T(8,128)(2,1)S(1)}, bf16[8,32,128]{2,1,0:T(8,128)(2,1)S(1)}, u32[]{:S(2)}, u32[]{:S(2)}) collective-permute-start(bf16[8,32,128]{2,1,0:T(8,128)(2,1)S(1)} %copy-done.4), channel_id=1, source_target_pairs={{0,8},{8,16},{16,24},{24,0},{1,9},{9,17},{17,25},{25,1},{2,10},{10... | collective-permute-start | bytes 196616 | tf_op jit(solution)/shard_map/ppermute | solution.py:506
  45.7 2.2 %copy-start = (f32[32,256,128]{2,1,0:T(8,128)S(1)}, f32[32,256,128]{2,1,0:T(8,128)}, u32[]{:S(2)}) copy-start(f32[32,256,128]{2,1,0:T(8,128)} %design_ref.3) | copy-start | bytes 12582916
  55.9 29.4 %copy-start.1 = (s32[16,16]{1,0:T(8,128)S(1)}, s32[16,16]{1,0:T(8,128)}, u32[]{:S(2)}) copy-start(s32[16,16]{1,0:T(8,128)} %elements_ref.1) | copy-start | bytes 3076
  55.9 29.4 %copy-start.3 = (s32[1,16]{1,0:T(1,128)S(1)}, s32[1,16]{1,0:T(1,128)}, u32[]{:S(2)}) copy-start(s32[1,16]{1,0:T(1,128)} %counts_ref.3) | copy-start | bytes 196
  55.9 5.0 %collective-permute-start.4 = (bf16[32,8,256]{2,1,0:T(8,128)(2,1)S(1)}, bf16[32,8,256]{2,1,0:T(8,128)(2,1)S(1)}, u32[]{:S(2)}, u32[]{:S(2)}) collective-permute-start(bf16[32,8,256]{2,1,0:T(8,128)(2,1)S(1)} %get-tuple-element.22), channel_id=1, source_target_pairs={{0,1},{1,0},{2,3},{3,2},{4,5},{5,4},{6,7},{7,6},{8,9},{9,8},{10,11... | collective-permute-start | bytes 393224 | tf_op jit(solution)/shard_map/ppermute | solution.py:547
  62.1 3.7 %collective-permute-start.5 = (bf16[32,8,128]{2,1,0:T(8,128)(2,1)S(1)}, bf16[32,8,128]{2,1,0:T(8,128)(2,1)S(1)}, u32[]{:S(2)}, u32[]{:S(2)}) collective-permute-start(bf16[32,8,128]{2,1,0:T(8,128)(2,1)S(1)} %get-tuple-element.24), channel_id=1, source_target_pairs={{0,2},{2,4},{4,6},{6,0},{1,3},{3,5},{5,7},{7,1},{8,10},{10,12},{12... | collective-permute-start | bytes 196616 | tf_op jit(solution)/shard_map/ppermute | solution.py:559
  62.2 3.7 %collective-permute-start.6 = (bf16[32,8,128]{2,1,0:T(8,128)(2,1)S(1)}, bf16[32,8,128]{2,1,0:T(8,128)(2,1)S(1)}, u32[]{:S(2)}, u32[]{:S(2)}) collective-permute-start(bf16[32,8,128]{2,1,0:T(8,128)(2,1)S(1)} %get-tuple-element.25), channel_id=1, source_target_pairs={{2,0},{4,2},{6,4},{0,6},{3,1},{5,3},{7,5},{1,7},{10,8},{12,10},{14... | collective-permute-start | bytes 196616 | tf_op jit(solution)/shard_map/ppermute | solution.py:560
where the time goes:
time: 87.5 us; the launch traced here: 87.1 us
  waiting for transfers between devices  29.6 us (34%)
  Pallas kernels  26.7 us (31%)
  starting transfers between devices  16.7 us (19%)
  blocking collectives  10.4 us (12%)
  local copies, waits for them, and re-layouts  2.29 us (3%)
    ppermute x1, waiting for transfers between devices, update(): high_edge = lax.ppermute(down_edge, 'tx', down)  21.8 us
    all_to_all x1, blocking collectives, update(): lax.all_to_all(ratios, ('tx', 'ty'), split_axis=0, concat_axis=0, tiled=T...  10.4 us
    pallas_call x1, Pallas kernels, update(): pl.pallas_call(functools.partial(finish_kernel, float(TAPS ** 4)), out_sh...  8.9 us
    pallas_call x1, Pallas kernels, update(): pl.pallas_call(functools.partial(deposit_kernel, cells_y, slots), out_sha...  7.92 us
    all_to_all x1, starting transfers between devices, update(): lax.all_to_all(payload, ('tx', 'ty'), split_axis=0, concat_axis=0, tiled=...  7.56 us
    pallas_call x1, Pallas kernels, update(): pl.pallas_call(functools.partial(pack_kernel, n_ty), out_shape=(shape((ti...  4.28 us
    ppermute x1, waiting for transfers between devices, update(): rim = lax.ppermute(rim, 'gz', [(0, 1), (1, 0)])  3.55 us
    pallas_call x1, Pallas kernels, update(): up_main, down_main = call(design, up_edge)  2.57 us
  transfers between devices with their start and end apart: 8, of which 4 were waited for; matrix products, arithmetic and copies ran while one was open for 0% of the time, Pallas kernels for 13%

commit v1 on v0

--- a/solution.py
+++ b/solution.py
@@ -43,8 +43,14 @@
     )
 
 
-def picker(first):
+def picker():
+    first = jnp.where(lax.axis_index("gz") == 0, LANES - RADIUS, 0)
     return onehot(iota((RADIUS, LANES), 1) == iota((RADIUS, LANES), 0) + first)
+
+
+def side_weights():
+    first = jnp.where(lax.axis_index("gz") == 0, LANES, -RADIUS)
+    return cone(iota((RADIUS, LANES), 0) + first - iota((RADIUS, LANES), 1))
 
 
 def running(planes, length):
@@ -65,31 +71,23 @@
 
 
 def pack_kernel(
-    n_ty, counts_ref, quad_ref, zoff_ref, basis_hbm, forward_hbm, adjoint_hbm, weights_hbm,
-    elements_hbm, blocks_hbm, design_ref, pay_ref, up_edge_ref, down_edge_ref, basis_ref,
-    forward_ref, adjoint_ref, weights_ref, elements_ref, blocks_ref, strip_ref, code_ref, sem,
+    n_ty, cells_x, cells_y, counts_hbm, quad_hbm, basis_hbm, forward_hbm, adjoint_hbm, weights_hbm,
+    elements_hbm, blocks_hbm, pay_ref, basis_ref, forward_ref, adjoint_ref, weights_ref,
+    elements_ref, blocks_ref, counts_ref, quad_ref, code_ref, sem,
 ):
     sources = (forward_hbm, adjoint_hbm, basis_hbm, elements_hbm, blocks_hbm, weights_hbm)
+    sources += (counts_hbm, quad_hbm)
     targets = (forward_ref, adjoint_ref, basis_ref, elements_ref, blocks_ref, weights_ref)
+    targets += (counts_ref, quad_ref)
     loads = [
-        pltpu.make_async_copy(source, target, sem.at[2 + i])
+        pltpu.make_async_copy(source, target, sem.at[i])
         for i, (source, target) in enumerate(zip(sources, targets))
     ]
     for load in loads:
         load.start()
-    cells_x, cells_y, _ = design_ref.shape
     tiles, capacity = elements_ref.shape
     points = quad_ref.shape[0]
     highest = lax.Precision.HIGHEST
-    copies = [
-        pltpu.make_async_copy(
-            design_ref.at[pl.ds(start, RADIUS)], strip_ref.at[pl.ds(side * RADIUS, RADIUS)],
-            sem.at[side],
-        )
-        for side, start in enumerate((0, cells_x - RADIUS))
-    ]
-    for copy in copies:
-        copy.start()
     for load in loads:
         load.wait()
 
@@ -159,7 +157,24 @@
             pay_ref[t, order * capacity : (order + 1) * capacity, :] = weights_ref[source]
         pay_ref[t, 3 * capacity :, :] = meta.astype(BF16)
 
-    pick = picker(zoff_ref[0])
+
+def strips(design_ref, strip_ref, sem):
+    cells_x = design_ref.shape[0]
+    return [
+        pltpu.make_async_copy(
+            design_ref.at[pl.ds(start, RADIUS)], strip_ref.at[pl.ds(side * RADIUS, RADIUS)],
+            sem.at[side],
+        )
+        for side, start in enumerate((0, cells_x - RADIUS))
+    ]
+
+
+def cast_edge_kernel(design_ref, token_ref, up_edge_ref, down_edge_ref, strip_ref, sem):
+    cells_y = design_ref.shape[1]
+    copies = strips(design_ref, strip_ref, sem)
+    for copy in copies:
+        copy.start()
+    pick = picker()
     for side, edge_ref in enumerate((down_edge_ref, up_edge_ref)):
         copies[side].wait()
 
@@ -174,15 +189,9 @@
                 edge_ref[p, start : start + RADIUS] = flipped[:, k * LANES : (k + 1) * LANES]
 
 
-def main_kernel(design_ref, token_ref, up_ref, down_ref, strip_ref, sem):
-    cells_x, cells_y, _ = design_ref.shape
-    copies = [
-        pltpu.make_async_copy(
-            design_ref.at[pl.ds(start, RADIUS)], strip_ref.at[pl.ds(side * RADIUS, RADIUS)],
-            sem.at[side],
-        )
-        for side, start in enumerate((0, cells_x - RADIUS))
-    ]
+def cast_main_kernel(design_ref, token_ref, up_ref, down_ref, strip_ref, sem):
+    cells_y = design_ref.shape[1]
+    copies = strips(design_ref, strip_ref, sem)
     for copy in copies:
         copy.start()
     for side, main_ref in enumerate((down_ref, up_ref)):
@@ -195,7 +204,7 @@
 
 
 def deposit_kernel(
-    cells_y, slots, zoff_ref, design_ref, low_ref, high_ref, pay_ref, grid_ref, rows_out_ref,
+    cells_y, slots, design_ref, low_ref, high_ref, pay_ref, grid_ref, rows_out_ref,
     rim_ref, own_ref, flip_ref, weight_ref, code_ref, value_ref, code_smem, value_smem, sem,
 ):
     cells_x = design_ref.shape[0] // cells_y
@@ -252,7 +261,7 @@
                 grid_ref[pl.ds(row, 1), :] = grid_ref[pl.ds(row, 1), :] + amount
 
     total = cells_x + 2 * RADIUS
-    pick = picker(zoff_ref[0])
+    pick = picker()
 
     @pl.loop(0, cells_x, unroll=4)
     def _(x):
@@ -293,12 +302,12 @@
         rim_ref[i] = value.astype(BF16)
 
 
-def edge_kernel(zoff_ref, rows_ref, rim_ref, first_ref, last_ref):
+def edge_kernel(rows_ref, rim_ref, first_ref, last_ref):
     cells_x, double, cells_z = rows_ref.shape
     cells_y = rim_ref.shape[2]
     weights = cone(iota((cells_z, cells_z), 0) - iota((cells_z, cells_z), 1))
     weights = jnp.concatenate([weights, weights], axis=0)
-    side = cone(iota((RADIUS, cells_z), 0) + zoff_ref[1] - iota((RADIUS, cells_z), 1))
+    side = side_weights()
     rows = rows_ref[...].reshape(cells_x * double, cells_z)
     value = dot(jnp.concatenate(halves(rows), axis=1), weights)
     for x in range(cells_x):
@@ -310,87 +319,129 @@
             out_ref[x] = (value[at : at + RADIUS] + dot(rim, side, TN)).astype(BF16)
 
 
+STEP = 8
+
+
+def project_planes(
+    scale_total, depth, places, smooth_ref, rim_ref, ends_ref, proj_ref, done
+):
+    _, _, cells_y = rim_ref.shape
+    cells_z = proj_ref.shape[1]
+    across = cone(iota((cells_y, cells_y), 0) - iota((cells_y, cells_y), 1))
+    along = cone(iota((cells_z, cells_z), 0) - iota((cells_z, cells_z), 1))
+    along = jnp.concatenate([along, side_weights()], axis=0)
+    z = iota((1, cells_z), 1) + lax.axis_index("gz") * cells_z
+    inside = jnp.zeros((1, cells_z), F32)
+    for offset in range(-RADIUS, RADIUS + 1):
+        good = (z + offset >= 0) & (z + offset < depth)
+        inside = inside + jnp.where(good, float(TAPS - abs(offset)), 0.0)
+    scale = 8.0 / (scale_total * inside)
+    top = math.tanh(4.0)
+
+    @pl.loop(0, places[1])
+    def _(g):
+        base = places[0] + g * places[2]
+        rims = rim_ref[pl.ds(base, STEP)].reshape(STEP * RADIUS, cells_y)
+        rims = dot(rims, across)
+        for pair in range(STEP // 2):
+            both = [smooth_ref[g * STEP + 2 * pair + k] for k in range(2)]
+            both = dot(across, jnp.concatenate(both, axis=1)).astype(BF16)
+            for k in range(2):
+                x = base + 2 * pair + k
+                at = (2 * pair + k) * RADIUS
+                flipped = rims[at : at + RADIUS].T.astype(BF16)
+                half = both[:, k * cells_z : (k + 1) * cells_z]
+                value = dot(jnp.concatenate([half, flipped], axis=1), along)
+                spot = pl.ds(pl.multiple_of(x * RADIUS, RADIUS), RADIUS)
+                first = value[:RADIUS] + ends_ref[0, spot, :]
+                last = value[cells_y - RADIUS :] + ends_ref[1, spot, :]
+                value = jnp.concatenate([first, value[RADIUS : cells_y - RADIUS], last], axis=0)
+                value = (top + jnp.tanh(value * scale)) * (1.0 / (2.0 * top))
+                proj_ref[pl.ds(pl.multiple_of(x * cells_y, 8), cells_y), :] = value
+        done(g)
+
+
+def inner_kernel(
+    scale_total, depth, grid_ref, rim_ref, before_ref, after_ref, proj_ref, ends_ref, smooth_ref
+):
+    cells_x, _, cells_y = rim_ref.shape
+    cells_z = proj_ref.shape[1]
+    many = cells_x * RADIUS
+    row, column = iota((many, many), 0), iota((many, many), 1)
+    same = row // RADIUS == column // RADIUS
+    gap = row % RADIUS - column % RADIUS
+    for rows_in_ref, distance, index in ((before_ref, gap + RADIUS, 0), (after_ref, gap - RADIUS, 1)):
+        weights = jnp.where(same, cone(distance).astype(F32), 0.0).astype(BF16)
+        ends_ref[index] = dot(weights, rows_in_ref[...].reshape(many, cells_z))
+    count = cells_x - 2 * RADIUS
+    chunk = 16
+
+    @pl.loop(0, cells_y // chunk)
+    def _(j):
+        start = pl.multiple_of(j * chunk, chunk)
+        planes = []
+        for e in range(RADIUS, RADIUS + cells_x):
+            at = pl.multiple_of(e * cells_y + start, chunk)
+            planes.append(clipped(grid_ref[pl.ds(at, chunk), :] - 0.5))
+        for i, value in enumerate(running(planes, count)):
+            smooth_ref[i, pl.ds(start, chunk), :] = value.astype(BF16)
+
+    project_planes(
+        scale_total, depth, (RADIUS, count // STEP, STEP), smooth_ref, rim_ref, ends_ref,
+        proj_ref, lambda g: None,
+    )
+
+
 def finish_kernel(
-    scale_total, zoff_ref, own_ref, grid_ref, low_ref, high_ref, rim_ref, before_ref, after_ref,
-    pay_ref, out_ref, ratio_ref, rims_ref, smooth_ref, proj_ref, picked_ref, rows_ref, sem, own_sem,
+    scale_total, depth, inner_ref, own_ref, grid_ref, low_ref, high_ref, rim_ref, ends_ref,
+    pay_ref, proj_ref, out_ref, ratio_ref, pad_ref, smooth_ref, picked_ref, rows_ref, sem, own_sem,
 ):
     cells_x, _, cells_y = rim_ref.shape
     cells_z = out_ref.shape[1]
     partners = pay_ref.shape[0]
     capacity = picked_ref.shape[0] // partners
-    total = cells_x + 2 * RADIUS
-    inner = cells_y - 2 * RADIUS
     chunk = 16
     fetch = pltpu.make_async_copy(own_ref, rows_ref, own_sem)
     fetch.start()
 
-    for source_ref, base, into in ((low_ref, 0, 0), (high_ref, RADIUS + cells_x, RADIUS)):
-        @pl.loop(0, RADIUS)
-        def _(p):
-            at = pl.multiple_of((base + p) * cells_y, 8)
-            to = pl.multiple_of((into + p) * cells_y, 8)
-            main = grid_ref[pl.ds(at + RADIUS, inner), :] + source_ref[p].astype(F32)
-            rims_ref[pl.ds(to + RADIUS, inner), :] = clipped(main)
-            for start in (0, cells_y - RADIUS):
-                value = grid_ref[pl.ds(at + start, RADIUS), :]
-                rims_ref[pl.ds(to + start, RADIUS), :] = clipped(value)
+    def send(first, count, index):
+        rows = pl.ds(pl.multiple_of(first * cells_y, 8), count * cells_y)
+        return pltpu.make_async_copy(proj_ref.at[rows], out_ref.at[rows], sem.at[index])
+
+    inner_send = send(RADIUS, cells_x - 2 * RADIUS, 2)
+    inner_send.start()
+    for p in range(RADIUS):
+        pad_ref[p, RADIUS : cells_y - RADIUS, :] = low_ref[p]
+        pad_ref[RADIUS + p, RADIUS : cells_y - RADIUS, :] = high_ref[p]
 
     @pl.loop(0, cells_y // chunk)
     def _(j):
-        planes = []
         start = pl.multiple_of(j * chunk, chunk)
-        for e in range(total):
-            if RADIUS <= e < RADIUS + cells_x:
-                at = pl.multiple_of(e * cells_y + start, chunk)
-                value = clipped(grid_ref[pl.ds(at, chunk), :] - 0.5)
-            else:
-                side = e if e < RADIUS else e - cells_x
-                value = rims_ref[pl.ds(pl.multiple_of(side * cells_y + start, chunk), chunk), :]
-            planes.append(value)
-        for i, value in enumerate(running(planes, cells_x)):
+        row = start + iota((chunk, 1), 0)
+        main = (row >= RADIUS) & (row < cells_y - RADIUS)
+
+        def own(e):
+            at = pl.multiple_of(e * cells_y + start, chunk)
+            return clipped(grid_ref[pl.ds(at, chunk), :] - 0.5)
+
+        def outer(e, p):
+            at = pl.multiple_of(e * cells_y + start, chunk)
+            rim = pad_ref[p, pl.ds(start, chunk), :].astype(F32)
+            return clipped(grid_ref[pl.ds(at, chunk), :] + jnp.where(main, rim, 0.0))
+
+        planes = [outer(e, e) for e in range(RADIUS)]
+        planes += [own(e) for e in range(RADIUS, 3 * RADIUS)]
+        for i, value in enumerate(running(planes, RADIUS)):
             smooth_ref[i, pl.ds(start, chunk), :] = value.astype(BF16)
-
-    across = cone(iota((cells_y, cells_y), 0) - iota((cells_y, cells_y), 1))
-    along = cone(iota((cells_z, cells_z), 0) - iota((cells_z, cells_z), 1))
-    along = jnp.concatenate([along, along], axis=0)
-    side = cone(iota((RADIUS, cells_z), 0) + zoff_ref[1] - iota((RADIUS, cells_z), 1))
-    column = iota((cells_y, 2 * RADIUS), 1)
-    place = jnp.where(column < RADIUS, column - RADIUS, column - RADIUS + cells_y)
-    edge = cone(place - iota((cells_y, 2 * RADIUS), 0))
-    z = iota((1, cells_z), 1) + zoff_ref[2]
-    inside = jnp.zeros((1, cells_z), F32)
-    for offset in range(-RADIUS, RADIUS + 1):
-        good = (z + offset >= 0) & (z + offset < zoff_ref[3])
-        inside = inside + jnp.where(good, float(TAPS - abs(offset)), 0.0)
-    scale = 8.0 / (scale_total * inside)
-    top = math.tanh(4.0)
-    step = 4
-
-    def copy(g):
-        rows = pl.ds(pl.multiple_of(g * step * cells_y, 8), step * cells_y)
-        return pltpu.make_async_copy(proj_ref.at[rows], out_ref.at[rows], sem.at[g])
-
-    @pl.loop(0, cells_x // step)
-    def _(g):
-        rims = rim_ref[pl.ds(g * step, step)].reshape(step * RADIUS, cells_y)
-        rims = dot(rims, across).astype(BF16)
-        for pair in range(step // 2):
-            x = g * step + 2 * pair
-            both = jnp.concatenate([smooth_ref[x], smooth_ref[x + 1]], axis=1)
-            both = dot(across, both)
-            for k in range(2):
-                half = jnp.concatenate(halves(both[:, k * cells_z : (k + 1) * cells_z]), axis=1)
-                value = dot(half, along)
-                at = (2 * pair + k) * RADIUS
-                value = value + dot(rims[at : at + RADIUS], side, TN)
-                ends = jnp.concatenate(
-                    [before_ref[x + k].astype(F32), after_ref[x + k].astype(F32)], axis=0
-                ).astype(BF16)
-                value = value + dot(edge, ends)
-                value = (top + jnp.tanh(value * scale)) * (1.0 / (2.0 * top))
-                proj_ref[pl.ds(pl.multiple_of((x + k) * cells_y, 8), cells_y), :] = value
-        copy(g).start()
-
+        planes = [own(e) for e in range(cells_x - RADIUS, cells_x + RADIUS)]
+        planes += [outer(cells_x + RADIUS + p, RADIUS + p) for p in range(RADIUS)]
+        for i, value in enumerate(running(planes, RADIUS)):
+            smooth_ref[RADIUS + i, pl.ds(start, chunk), :] = value.astype(BF16)
+
+    project_planes(
+        scale_total, depth, (0, 2, cells_x - RADIUS), smooth_ref, rim_ref, ends_ref, proj_ref,
+        lambda g: send(g * (cells_x - RADIUS), RADIUS, g).start(),
+    )
     fetch.wait()
 
     @pl.loop(0, partners)
@@ -410,24 +461,43 @@
         amount = dot(ones, high, NT) + dot(ones, low, NT)
         ratio_ref[pl.ds(c, 1), :] = (amount / dot(ones, w, NT))[:1]
 
-    @pl.loop(0, cells_x // step)
-    def _(g):
-        copy(g).wait()
+    for g in range(2):
+        send(g * (cells_x - RADIUS), RADIUS, g).wait()
+    inner_send.wait()
 
 
 def back_kernel(counts_ref, elements_ref, ratio_ref, out_ref):
     tiles, capacity = elements_ref.shape
     high_count = out_ref.shape[0]
-    total = jnp.zeros(out_ref.shape, F32)
-    for t in range(tiles):
-        element = elements_ref[pl.ds(t, 1), :]
-        live = iota((1, capacity), 1) < counts_ref[0, t]
-        ratio = jnp.where(live, ratio_ref[pl.ds(t, 1), :], 0.0)
-        lane = onehot(iota((LANES, capacity), 0) == (element & (LANES - 1)))
-        spread = jnp.where(iota((high_count, capacity), 0) == element // LANES, ratio, 0.0)
-        high, low = halves(spread)
-        total = total + (dot(high, lane, NT) + dot(low, lane, NT))
-    out_ref[...] = total
+    group = min(tiles, 16)
+    wide = group * capacity
+    out_ref[...] = jnp.zeros(out_ref.shape, F32)
+
+    @pl.loop(0, tiles // group)
+    def _(g):
+        start = pl.multiple_of(g * group, group)
+        element = elements_ref[pl.ds(start, group), :]
+        tile = iota((group, tiles), 0) + start == iota((group, tiles), 1)
+        counts = jnp.where(tile, counts_ref[...].astype(F32), 0.0)
+        counts = jnp.sum(counts, axis=1, keepdims=True)
+        live = iota((group, capacity), 1).astype(F32) < counts
+        ratio = jnp.where(live, ratio_ref[pl.ds(start, group), :], 0.0)
+        first, _ = halves(ratio)
+        second, third = halves(ratio - first.astype(F32))
+        parts = [(element // LANES).astype(F32), (element % LANES).astype(F32)]
+        parts += [part.astype(F32) for part in (first, second, third)]
+        spread = onehot(iota((capacity, wide), 1) % capacity == iota((capacity, wide), 0))
+        own = iota((group, wide), 1) // capacity == iota((group, wide), 0)
+        rows = []
+        for part in parts:
+            part = jnp.where(own, dot(part.astype(BF16), spread), 0.0)
+            rows.append(jnp.sum(part, axis=0, keepdims=True))
+        lane = onehot(iota((LANES, wide), 0).astype(F32) == rows[1])
+        mine = iota((high_count, wide), 0).astype(F32) == rows[0]
+        total = jnp.zeros(out_ref.shape, F32)
+        for part in rows[2:]:
+            total = total + dot(jnp.where(mine, part, 0.0).astype(BF16), lane, NT)
+        out_ref[...] = out_ref[...] + total
 
 
 def update(
@@ -449,32 +519,19 @@
     slots = 3 * capacity
     edge_count, elements = forward_edges.shape[1:]
     rows_ext = (cells_x + 2 * RADIUS) * cells_y
-    gz = lax.axis_index("gz")
-    zoff = jnp.stack(
-        [
-            jnp.where(gz == 0, cells_z - RADIUS, 0),
-            jnp.where(gz == 0, cells_z, -RADIUS),
-            gz * cells_z,
-            jnp.int32(n_gz * cells_z),
-        ]
-    ).astype(jnp.int32)
     whole = pl.BlockSpec(memory_space=VMEM)
-    scalars = pl.BlockSpec(memory_space=SMEM)
     anywhere = pl.BlockSpec(memory_space=pltpu.HBM)
     shape = jax.ShapeDtypeStruct
+    stay = lambda x: pltpu.with_memory_space_constraint(x, pltpu.HBM)
     params = lambda mib: pltpu.CompilerParams(vmem_limit_bytes=mib << 20)
 
     inner = cells_y - 2 * RADIUS
     edge_rows = 2 * RADIUS + RADIUS * cells_y // LANES
-    payload, up_edge, down_edge = pl.pallas_call(
-        functools.partial(pack_kernel, n_ty),
-        out_shape=(
-            shape((tiles, slots + 8, LANES), BF16),
-            shape((RADIUS, edge_rows, LANES), BF16),
-            shape((RADIUS, edge_rows, LANES), BF16),
-        ),
-        in_specs=[scalars] * 3 + [anywhere] * 7,
-        out_specs=(whole,) * 3,
+    payload = pl.pallas_call(
+        functools.partial(pack_kernel, n_ty, cells_x, cells_y),
+        out_shape=shape((tiles, slots + 8, LANES), BF16),
+        in_specs=[anywhere] * 8,
+        out_specs=whole,
         scratch_shapes=[
             VMEM(edge_basis.shape[::-1], F32),
             VMEM((edge_count, 2, elements), F32),
@@ -482,42 +539,46 @@
             VMEM(slot_weights.shape, BF16),
             VMEM(slot_elements.shape, jnp.int32),
             VMEM(slot_blocks.shape, jnp.int32),
-            VMEM((2 * RADIUS, cells_y, cells_z), F32),
+            SMEM(slot_counts.shape, jnp.int32),
+            SMEM(quad_weights.shape, F32),
             VMEM((4, tiles, LANES), F32),
             pltpu.SemaphoreType.DMA((8,)),
         ],
+        compiler_params=params(24),
         name="pack",
     )(
-        slot_counts,
-        quad_weights,
-        zoff,
-        edge_basis.T,
-        forward_edges.transpose(1, 0, 2),
-        adjoint_edges.transpose(1, 0, 2),
-        slot_weights,
-        slot_elements,
-        slot_blocks,
-        design,
+        stay(slot_counts),
+        stay(quad_weights),
+        stay(edge_basis.T),
+        stay(forward_edges.transpose(1, 0, 2)),
+        stay(adjoint_edges.transpose(1, 0, 2)),
+        stay(slot_weights),
+        stay(slot_elements),
+        stay(slot_blocks),
     )
 
     arrived = lax.all_to_all(payload, ("tx", "ty"), split_axis=0, concat_axis=0, tiled=True)
     up = [(i, (i + 1) % n_tx) for i in range(n_tx)]
     down = [(t, s) for s, t in up]
+
+    def cast(kernel, rows, token):
+        strip = shape((RADIUS, rows, LANES), BF16)
+        return pl.pallas_call(
+            kernel,
+            out_shape=(strip, strip),
+            in_specs=[anywhere, anywhere],
+            out_specs=(whole, whole),
+            scratch_shapes=[
+                VMEM((2 * RADIUS, cells_y, cells_z), F32),
+                pltpu.SemaphoreType.DMA((2,)),
+            ],
+            compiler_params=params(16),
+        )(stay(design), token)
+
+    up_edge, down_edge = cast(cast_edge_kernel, edge_rows, stay(payload))
     low_edge = lax.ppermute(up_edge, "tx", up)
     high_edge = lax.ppermute(down_edge, "tx", down)
-    main = shape((RADIUS, inner, LANES), BF16)
-    call = pl.pallas_call(
-        main_kernel,
-        out_shape=(main, main),
-        in_specs=[anywhere, anywhere],
-        out_specs=(whole, whole),
-        scratch_shapes=[
-            VMEM((2 * RADIUS, cells_y, cells_z), F32),
-            pltpu.SemaphoreType.DMA((2,)),
-        ],
-        name="main_rims",
-    )
-    up_main, down_main = call(design, up_edge)
+    up_main, down_main = cast(cast_main_kernel, inner, up_edge)
     low_main = lax.ppermute(up_main, "tx", up)
     high_main = lax.ppermute(down_main, "tx", down)
 
@@ -529,7 +590,7 @@
             shape((cells_x, RADIUS, cells_y), BF16),
             shape((tiles, LANES), jnp.int32),
         ),
-        in_specs=[scalars, anywhere] + [whole] * 3,
+        in_specs=[anywhere] + [whole] * 3,
         out_specs=(whole,) * 4,
         scratch_shapes=[
             VMEM((cells_x + 2 * RADIUS, RADIUS, cells_y), F32),
@@ -542,50 +603,59 @@
         ],
         compiler_params=params(16),
         name="deposit",
-    )(zoff, design.reshape(cells_x * cells_y, cells_z), low_edge, high_edge, arrived)
+    )(stay(design.reshape(cells_x * cells_y, cells_z)), low_edge, high_edge, arrived)
 
     rim = lax.ppermute(rim, "gz", [(0, 1), (1, 0)])
     edge = shape((cells_x, RADIUS, cells_z), BF16)
     first, last = pl.pallas_call(
         edge_kernel,
         out_shape=(edge, edge),
-        in_specs=[scalars, whole, whole],
+        in_specs=[whole, whole],
         out_specs=(whole, whole),
         compiler_params=params(16),
         name="edges",
-    )(zoff, edge_smooth, rim)
+    )(edge_smooth, rim)
     up = [(i, (i + 1) % n_ty) for i in range(n_ty)]
     down = [(t, s) for s, t in up]
     before = lax.ppermute(last, "ty", up)
     after = lax.ppermute(first, "ty", down)
 
-    projected, ratios = pl.pallas_call(
-        functools.partial(finish_kernel, float(TAPS**4)),
-        out_shape=(
-            shape((cells_x * cells_y, cells_z), F32),
-            shape((tiles * capacity // LANES, LANES), F32),
-        ),
-        in_specs=[scalars] + [whole] * 8,
-        out_specs=(anywhere, whole),
+    flat = shape((cells_x * cells_y, cells_z), F32)
+    constants = (float(TAPS**4), n_gz * cells_z)
+    call = pl.pallas_call(
+        functools.partial(inner_kernel, *constants),
+        out_shape=(flat, shape((2, cells_x * RADIUS, cells_z), F32)),
+        in_specs=[whole] * 4,
+        out_specs=(whole, whole),
+        scratch_shapes=[VMEM((cells_x - 2 * RADIUS, cells_y, cells_z), BF16)],
+        compiler_params=params(16),
+        name="inner",
+    )
+    partial, ends = call(grid, rim, before, after)
+    _, projected, ratios = pl.pallas_call(
+        functools.partial(finish_kernel, *constants),
+        out_shape=(flat, flat, shape((tiles * capacity // LANES, LANES), F32)),
+        in_specs=[whole] * 8,
+        out_specs=(whole, anywhere, whole),
         scratch_shapes=[
-            VMEM((2 * RADIUS * cells_y, cells_z), F32),
-            VMEM((cells_x, cells_y, cells_z), BF16),
-            VMEM((cells_x * cells_y, cells_z), F32),
+            VMEM((2 * RADIUS, cells_y, cells_z), BF16),
+            VMEM((2 * RADIUS, cells_y, cells_z), BF16),
             VMEM((tiles * capacity, cells_z), F32),
             SMEM((tiles, LANES), jnp.int32),
-            pltpu.SemaphoreType.DMA((cells_x // 4,)),
+            pltpu.SemaphoreType.DMA((3,)),
             pltpu.SemaphoreType.DMA,
         ],
-        compiler_params=params(24),
+        input_output_aliases={0: 0},
+        compiler_params=params(16),
         name="finish",
-    )(zoff, rows_own, grid, low_main, high_main, rim, before, after, arrived)
+    )(partial, rows_own, grid, low_main, high_main, rim, ends, arrived)
 
     ratios = ratios.reshape(tiles, capacity)
     ratios = lax.all_to_all(ratios, ("tx", "ty"), split_axis=0, concat_axis=0, tiled=True)
     density = pl.pallas_call(
         back_kernel,
         out_shape=shape((elements // LANES, LANES), F32),
-        in_specs=[scalars, whole, whole],
+        in_specs=[whole] * 3,
         out_specs=whole,
         compiler_params=params(16),
         name="to_elements",

time: 87.5 us -> 79.8 us (0.912)
  Pallas kernels: 26.7 us -> 23 us
  local copies, waits for them, and re-layouts: 2.29 us -> 0.09 us
  waiting for transfers between devices: 29.6 us -> 28.5 us
    unnamed x12 -> x4, local copies, waits for them, and re-layouts: 2.21 us -> 0.01 us
    pallas_call x4 -> x6, Pallas kernels: 17 us -> 15.1 us  [the longest x1 4.57 us: update(): pl.pallas_call(functools.partial(finish_kernel, *constants), out_shape=(f...]
    pallas_call x1, Pallas kernels: 7.92 us -> 6.99 us  [update(): pl.pallas_call(functools.partial(deposit_kernel, cells_y, slots), out_sha...]
  transfers between devices with their start and end apart: 8 -> 8, of which waited for: 4 -> 4; matrix products, arithmetic and copies ran while one was open for 0% -> 0% of each run, Pallas kernels for 13% -> 18%
where the time goes in v1:
time: 79.8 us; the launch traced here: 79.5 us
  waiting for transfers between devices  28.5 us (36%)
  Pallas kernels  23 us (29%)
  starting transfers between devices  16.6 us (21%)
  blocking collectives  10.6 us (13%)
    ppermute x1, waiting for transfers between devices, update(): high_edge = lax.ppermute(down_edge, 'tx', down)  21.5 us
    all_to_all x1, blocking collectives, update(): lax.all_to_all(ratios, ('tx', 'ty'), split_axis=0, concat_axis=0, tiled=T...  10.6 us
    all_to_all x1, starting transfers between devices, update(): lax.all_to_all(payload, ('tx', 'ty'), split_axis=0, concat_axis=0, tiled=...  7.43 us
    pallas_call x1, Pallas kernels, update(): pl.pallas_call(functools.partial(deposit_kernel, cells_y, slots), out_sha...  6.99 us
    pallas_call x1, Pallas kernels, update(): pl.pallas_call(functools.partial(finish_kernel, *constants), out_shape=(f...  4.57 us
    pallas_call x2, Pallas kernels, cast(): pl.pallas_call(kernel, out_shape=(strip, strip), in_specs=[anywhere, anyw...  3.62 us
    ppermute x1, waiting for transfers between devices, update(): rim = lax.ppermute(rim, 'gz', [(0, 1), (1, 0)])  3.55 us
    pallas_call x1, Pallas kernels, update(): partial, ends = call(grid, rim, before, after)  3.34 us
  transfers between devices with their start and end apart: 8, of which 4 were waited for; matrix products, arithmetic and copies ran while one was open for 0% of the time, Pallas kernels for 18%

profile of v1, /device:TPU:0, one launch (start us, length us, event | category | flops | bytes accessed | tf_op | source)
XLA Modules:
  0.0 79.5 jit_solution(17575411561278569831)
XLA Ops:
  0.6 2.8 %pack.1.token_ref = bf16[16,56,128]{2,1,0:T(8,128)(2,1)} custom-call(s32[1,16]{1,0:T(1,128)} %counts_ref.1, f32[8]{0:T(128)} %quad_hbm.1, f32[12,24]{1,0:T(8,128)} %bitcast.13, f32[12,2,2048]{2,1,0:T(2,128)} %bitcast.10, f32[12,2,2048]{2,1,0:T(2,128)} %bitcast.11, bf16[16,16,128]{2,1,0:T(8,128)(2,1)} %weights_hbm.1, s32[16,16]{1,0:T(8,128)} %elements_ref.1, ...), custom_call_target="tpu_custom_call" | custom-call | tf_op jit(solution)/shard_map/pack/pallas_call | solution.py:530
  3.5 7.4 %all-to-all-start = ((bf16[16,56,128]{2,1,0:T(8,128)(2,1)}), bf16[16,56,128]{2,1,0:T(8,128)(2,1)S(1)}, u32[]{:S(2)}, u32[]{:S(2)}) async-start(bf16[16,56,128]{2,1,0:T(8,128)(2,1)} %pack.1.token_ref), calls=%async_computation | async-start | bytes 458752 | tf_op jit(solution)/shard_map/all_to_all | solution.py:560
  10.9 2.0 %shard_map.104 = (bf16[8,32,128]{2,1,0:T(8,128)(2,1)S(1)}, bf16[8,32,128]{2,1,0:T(8,128)(2,1)S(1)}) custom-call(f32[32,256,128]{2,1,0:T(8,128)} %design_ref.3, bf16[16,56,128]{2,1,0:T(8,128)(2,1)} %pack.1.token_ref), custom_call_target="tpu_custom_call" | custom-call | tf_op jit(solution)/shard_map/pallas_call | solution.py:566
  12.9 1.6 %shard_map.105 = (bf16[8,240,128]{2,1,0:T(8,128)(2,1)S(1)}, bf16[8,240,128]{2,1,0:T(8,128)(2,1)S(1)}) custom-call(f32[32,256,128]{2,1,0:T(8,128)} %design_ref.3, bf16[8,32,128]{2,1,0:T(8,128)(2,1)S(1)} %get-tuple-element.16.token_ref), custom_call_target="tpu_custom_call" | custom-call | tf_op jit(solution)/shard_map/pallas_call | solution.py:566
  14.6 2.0 %collective-permute-start.5 = (bf16[8,240,128]{2,1,0:T(8,128)(2,1)S(1)}, bf16[8,240,128]{2,1,0:T(8,128)(2,1)S(1)}, u32[]{:S(2)}, u32[]{:S(2)}) collective-permute-start(bf16[8,240,128]{2,1,0:T(8,128)(2,1)S(1)} %get-tuple-element.25), channel_id=1, source_target_pairs={{0,8},{8,16},{16,24},{24,0},{1,9},{9,17},{17,25},{25,1},{2,10},{10... | collective-permute-start | bytes 1474568 | tf_op jit(solution)/shard_map/ppermute | solution.py:582
  16.5 1.9 %collective-permute-start.6 = (bf16[8,240,128]{2,1,0:T(8,128)(2,1)S(1)}, bf16[8,240,128]{2,1,0:T(8,128)(2,1)S(1)}, u32[]{:S(2)}, u32[]{:S(2)}) collective-permute-start(bf16[8,240,128]{2,1,0:T(8,128)(2,1)S(1)} %get-tuple-element.26), channel_id=1, source_target_pairs={{8,0},{16,8},{24,16},{0,24},{9,1},{17,9},{25,17},{1,25},{10,2},{18... | collective-permute-start | bytes 1474568 | tf_op jit(solution)/shard_map/ppermute | solution.py:583
  18.4 1.9 %collective-permute-start.1 = (bf16[8,32,128]{2,1,0:T(8,128)(2,1)S(1)}, bf16[8,32,128]{2,1,0:T(8,128)(2,1)S(1)}, u32[]{:S(2)}, u32[]{:S(2)}) collective-permute-start(bf16[8,32,128]{2,1,0:T(8,128)(2,1)S(1)} %get-tuple-element.17), channel_id=1, source_target_pairs={{8,0},{16,8},{24,16},{0,24},{9,1},{17,9},{25,17},{1,25},{10,2},{18... | collective-permute-start | bytes 196616 | tf_op jit(solution)/shard_map/ppermute | solution.py:580
  20.4 0.1 collective-permute-start
  20.5 21.5 %collective-permute-done.1.high_ref = bf16[8,32,128]{2,1,0:T(8,128)(2,1)S(1)} collective-permute-done((bf16[8,32,128]{2,1,0:T(8,128)(2,1)S(1)}, bf16[8,32,128]{2,1,0:T(8,128)(2,1)S(1)}, u32[]{:S(2)}, u32[]{:S(2)}) %collective-permute-start.1) | collective-permute-done | bytes 65568 | tf_op jit(solution)/shard_map/ppermute | solution.py:580
  42.0 1.5 %collective-permute-done.low_ref = bf16[8,32,128]{2,1,0:T(8,128)(2,1)S(1)} collective-permute-done((bf16[8,32,128]{2,1,0:T(8,128)(2,1)S(1)}, bf16[8,32,128]{2,1,0:T(8,128)(2,1)S(1)}, u32[]{:S(2)}, u32[]{:S(2)}) %collective-permute-start) | collective-permute-done | bytes 65568 | tf_op jit(solution)/shard_map/ppermute | solution.py:579
  43.5 0.0 all-to-all-done.pay_ref
  43.5 7.0 %deposit.1 = (f32[12288,128]{1,0:T(8,128)S(1)}, f32[32,16,128]{2,1,0:T(8,128)S(1)}, bf16[32,8,256]{2,1,0:T(8,128)(2,1)S(1)}, s32[16,128]{1,0:T(8,128)S(1)}) custom-call(f32[8192,128]{1,0:T(8,128)} %bitcast.9, bf16[8,32,128]{2,1,0:T(8,128)(2,1)S(1)} %collective-permute-done.low_ref, bf16[8,32,128]{2,1,0:T(8,128)(2,1)S(1)} %collective-permute-done.1.high_ref, ...), custom_call_target="tpu_custom_call" | custom-call | tf_op jit(solution)/shard_map/deposit/pallas_call | solution.py:585
  50.5 1.5 %collective-permute-start.2 = (bf16[32,8,256]{2,1,0:T(8,128)(2,1)S(1)}, bf16[32,8,256]{2,1,0:T(8,128)(2,1)S(1)}, u32[]{:S(2)}, u32[]{:S(2)}) collective-permute-start(bf16[32,8,256]{2,1,0:T(8,128)(2,1)S(1)} %get-tuple-element.19), channel_id=1, source_target_pairs={{0,1},{1,0},{2,3},{3,2},{4,5},{5,4},{6,7},{7,6},{8,9},{9,8},{10,11... | collective-permute-start | bytes 393224 | tf_op jit(solution)/shard_map/ppermute | solution.py:608
  52.0 3.6 %collective-permute-done.2.rim_ref = bf16[32,8,256]{2,1,0:T(8,128)(2,1)S(1)} collective-permute-done((bf16[32,8,256]{2,1,0:T(8,128)(2,1)S(1)}, bf16[32,8,256]{2,1,0:T(8,128)(2,1)S(1)}, u32[]{:S(2)}, u32[]{:S(2)}) %collective-permute-start.2) | collective-permute-done | bytes 131104 | tf_op jit(solution)/shard_map/ppermute | solution.py:608
  55.5 0.7 edges.1
  56.2 0.1 collective-permute-start.3
  56.3 1.7 %collective-permute-start.4 = (bf16[32,8,128]{2,1,0:T(8,128)(2,1)S(1)}, bf16[32,8,128]{2,1,0:T(8,128)(2,1)S(1)}, u32[]{:S(2)}, u32[]{:S(2)}) collective-permute-start(bf16[32,8,128]{2,1,0:T(8,128)(2,1)S(1)} %get-tuple-element.22), channel_id=1, source_target_pairs={{2,0},{4,2},{6,4},{0,6},{3,1},{5,3},{7,5},{1,7},{10,8},{12,10},{14... | collective-permute-start | bytes 196616 | tf_op jit(solution)/shard_map/ppermute | solution.py:621
  58.0 1.9 %collective-permute-done.3.before_ref = bf16[32,8,128]{2,1,0:T(8,128)(2,1)S(1)} collective-permute-done((bf16[32,8,128]{2,1,0:T(8,128)(2,1)S(1)}, bf16[32,8,128]{2,1,0:T(8,128)(2,1)S(1)}, u32[]{:S(2)}, u32[]{:S(2)}) %collective-permute-start.3) | collective-permute-done | bytes 65568 | tf_op jit(solution)/shard_map/ppermute | solution.py:620
  59.9 0.0 collective-permute-done.4.after_ref
  59.9 3.3 %inner.1 = (f32[8192,128]{1,0:T(8,128)S(1)}, f32[2,256,128]{2,1,0:T(8,128)S(1)}) custom-call(f32[12288,128]{1,0:T(8,128)S(1)} %get-tuple-element.18.grid_ref, bf16[32,8,256]{2,1,0:T(8,128)(2,1)S(1)} %collective-permute-done.2.rim_ref, bf16[32,8,128]{2,1,0:T(8,128)(2,1)S(1)} %collective-permute-done.3.before_ref, ...), custom_call_target="tpu_custom_call" | custom-call | tf_op jit(solution)/shard_map/inner/pallas_call | solution.py:634
  63.3 0.0 collective-permute-done.5.low_ref
  63.3 0.0 collective-permute-done.6.high_ref
  63.3 0.0 copy-start
  63.3 0.0 copy-start.1
  63.3 4.6 %finish.1 = (f32[8192,128]{1,0:T(8,128)S(1)}, f32[8192,128]{1,0:T(8,128)}, f32[2,128]{1,0:T(2,128)S(1)}) custom-call(f32[8192,128]{1,0:T(8,128)S(1)} %get-tuple-element.23.inner_ref, s32[16,128]{1,0:T(8,128)S(1)} %get-tuple-element.24.own_ref, f32[12288,128]{1,0:T(8,128)S(1)} %get-tuple-element.18.grid_ref, ...), custom_call_target="tpu_custom_call", output_to_operand_aliasing={{0}: (0, {})} | custom-call | tf_op jit(solution)/shard_map/finish/pallas_call | solution.py:635
  67.9 0.1 all_to_all.11
  68.0 10.6 %all_to_all.16 = f32[16,1,16]{2,1,0:T(1,128)S(1)} all-to-all(f32[16,1,16]{2,1,0:T(1,128)S(1)} %bitcast.12), channel_id=1, replica_groups=mesh['tx'=4,'ty'=4,'gz'=2] {'tx','ty'}, dimensions={0} | all-to-all | bytes 2048 | tf_op jit(solution)/shard_map/all_to_all | solution.py:654
  78.6 0.0 copy-done
  78.6 0.0 copy-done.1
  78.6 1.0 %to_elements.1 = f32[16,128]{1,0:T(8,128)} custom-call(s32[1,16]{1,0:T(1,128)S(1)} %copy-done.1, s32[16,16]{1,0:T(8,128)S(1)} %copy-done, f32[16,16]{1,0:T(8,128)S(1)} %bitcast.8), custom_call_target="tpu_custom_call" | custom-call | tf_op jit(solution)/shard_map/to_elements/pallas_call | solution.py:655
Async XLA Ops:
  3.5 40.0 %all-to-all-start = ((bf16[16,56,128]{2,1,0:T(8,128)(2,1)}), bf16[16,56,128]{2,1,0:T(8,128)(2,1)S(1)}, u32[]{:S(2)}, u32[]{:S(2)}) async-start(bf16[16,56,128]{2,1,0:T(8,128)(2,1)} %pack.1.token_ref), calls=%async_computation | async-start | bytes 458752 | tf_op jit(solution)/shard_map/all_to_all | solution.py:560
  14.6 48.7 %collective-permute-start.5 = (bf16[8,240,128]{2,1,0:T(8,128)(2,1)S(1)}, bf16[8,240,128]{2,1,0:T(8,128)(2,1)S(1)}, u32[]{:S(2)}, u32[]{:S(2)}) collective-permute-start(bf16[8,240,128]{2,1,0:T(8,128)(2,1)S(1)} %get-tuple-element.25), channel_id=1, source_target_pairs={{0,8},{8,16},{16,24},{24,0},{1,9},{9,17},{17,25},{25,1},{2,10},{10... | collective-permute-start | bytes 1474568 | tf_op jit(solution)/shard_map/ppermute | solution.py:582
  16.5 46.8 %collective-permute-start.6 = (bf16[8,240,128]{2,1,0:T(8,128)(2,1)S(1)}, bf16[8,240,128]{2,1,0:T(8,128)(2,1)S(1)}, u32[]{:S(2)}, u32[]{:S(2)}) collective-permute-start(bf16[8,240,128]{2,1,0:T(8,128)(2,1)S(1)} %get-tuple-element.26), channel_id=1, source_target_pairs={{8,0},{16,8},{24,16},{0,24},{9,1},{17,9},{25,17},{1,25},{10,2},{18... | collective-permute-start | bytes 1474568 | tf_op jit(solution)/shard_map/ppermute | solution.py:583
  18.4 23.5 %collective-permute-start.1 = (bf16[8,32,128]{2,1,0:T(8,128)(2,1)S(1)}, bf16[8,32,128]{2,1,0:T(8,128)(2,1)S(1)}, u32[]{:S(2)}, u32[]{:S(2)}) collective-permute-start(bf16[8,32,128]{2,1,0:T(8,128)(2,1)S(1)} %get-tuple-element.17), channel_id=1, source_target_pairs={{8,0},{16,8},{24,16},{0,24},{9,1},{17,9},{25,17},{1,25},{10,2},{18... | collective-permute-start | bytes 196616 | tf_op jit(solution)/shard_map/ppermute | solution.py:580
  20.4 23.1 %collective-permute-start = (bf16[8,32,128]{2,1,0:T(8,128)(2,1)S(1)}, bf16[8,32,128]{2,1,0:T(8,128)(2,1)S(1)}, u32[]{:S(2)}, u32[]{:S(2)}) collective-permute-start(bf16[8,32,128]{2,1,0:T(8,128)(2,1)S(1)} %get-tuple-element.16.token_ref), channel_id=1, source_target_pairs={{0,8},{8,16},{16,24},{24,0},{1,9},{9,17},{17,25},{25,1},{2,10},{10... | collective-permute-start | bytes 196616 | tf_op jit(solution)/shard_map/ppermute | solution.py:579
  50.5 5.0 %collective-permute-start.2 = (bf16[32,8,256]{2,1,0:T(8,128)(2,1)S(1)}, bf16[32,8,256]{2,1,0:T(8,128)(2,1)S(1)}, u32[]{:S(2)}, u32[]{:S(2)}) collective-permute-start(bf16[32,8,256]{2,1,0:T(8,128)(2,1)S(1)} %get-tuple-element.19), channel_id=1, source_target_pairs={{0,1},{1,0},{2,3},{3,2},{4,5},{5,4},{6,7},{7,6},{8,9},{9,8},{10,11... | collective-permute-start | bytes 393224 | tf_op jit(solution)/shard_map/ppermute | solution.py:608
  56.2 3.7 %collective-permute-start.3 = (bf16[32,8,128]{2,1,0:T(8,128)(2,1)S(1)}, bf16[32,8,128]{2,1,0:T(8,128)(2,1)S(1)}, u32[]{:S(2)}, u32[]{:S(2)}) collective-permute-start(bf16[32,8,128]{2,1,0:T(8,128)(2,1)S(1)} %get-tuple-element.21), channel_id=1, source_target_pairs={{0,2},{2,4},{4,6},{6,0},{1,3},{3,5},{5,7},{7,1},{8,10},{10,12},{12... | collective-permute-start | bytes 196616 | tf_op jit(solution)/shard_map/ppermute | solution.py:620
  56.3 3.7 %collective-permute-start.4 = (bf16[32,8,128]{2,1,0:T(8,128)(2,1)S(1)}, bf16[32,8,128]{2,1,0:T(8,128)(2,1)S(1)}, u32[]{:S(2)}, u32[]{:S(2)}) collective-permute-start(bf16[32,8,128]{2,1,0:T(8,128)(2,1)S(1)} %get-tuple-element.22), channel_id=1, source_target_pairs={{2,0},{4,2},{6,4},{0,6},{3,1},{5,3},{7,5},{1,7},{10,8},{12,10},{14... | collective-permute-start | bytes 196616 | tf_op jit(solution)/shard_map/ppermute | solution.py:621
  63.3 15.2 %copy-start = (s32[16,16]{1,0:T(8,128)S(1)}, s32[16,16]{1,0:T(8,128)}, u32[]{:S(2)}) copy-start(s32[16,16]{1,0:T(8,128)} %elements_ref.1) | copy-start | bytes 3076
  63.3 15.2 %copy-start.1 = (s32[1,16]{1,0:T(1,128)S(1)}, s32[1,16]{1,0:T(1,128)}, u32[]{:S(2)}) copy-start(s32[1,16]{1,0:T(1,128)} %counts_ref.1) | copy-start | bytes 196

commit v2 on v1

--- a/solution.py
+++ b/solution.py
@@ -12,12 +12,14 @@
 RADIUS = 8
 LANES = 128
 TAPS = RADIUS + 1
+STEP = 8
+NEAR = RADIUS // 2
+GROUP = 6
 F32 = jnp.float32
 BF16 = jnp.bfloat16
 SMEM = pltpu.SMEM
 VMEM = pltpu.VMEM
 NT = ((1,), (1,))
-TN = ((0,), (0,))
 
 
 def iota(shape, dim):
@@ -169,56 +171,49 @@
     ]
 
 
-def cast_edge_kernel(design_ref, token_ref, up_edge_ref, down_edge_ref, strip_ref, sem):
+def cast_kernel(
+    design_ref, token_ref, up_ref, down_ref, up_near_ref, down_near_ref, up_far_ref, down_far_ref,
+    strip_ref, sem,
+):
     cells_y = design_ref.shape[1]
+    edge_rows = 2 * RADIUS + RADIUS * cells_y // LANES
     copies = strips(design_ref, strip_ref, sem)
     for copy in copies:
         copy.start()
     pick = picker()
-    for side, edge_ref in enumerate((down_edge_ref, up_edge_ref)):
+    by_side = ((down_ref, down_near_ref, down_far_ref), (up_ref, up_far_ref, up_near_ref))
+    for side, targets in enumerate(by_side):
         copies[side].wait()
-
-        @pl.loop(0, RADIUS, unroll=4)
-        def _(p):
+        for p in range(RADIUS):
             plane = strip_ref[side * RADIUS + p] - 0.5
-            edge_ref[p, :RADIUS] = plane[:RADIUS].astype(BF16)
-            edge_ref[p, RADIUS : 2 * RADIUS] = plane[cells_y - RADIUS :].astype(BF16)
-            flipped = dot(pick, plane.astype(BF16), NT).astype(BF16)
-            for k in range(cells_y // LANES):
-                start = (2 + k) * RADIUS
-                edge_ref[p, start : start + RADIUS] = flipped[:, k * LANES : (k + 1) * LANES]
-
-
-def cast_main_kernel(design_ref, token_ref, up_ref, down_ref, strip_ref, sem):
-    cells_y = design_ref.shape[1]
-    copies = strips(design_ref, strip_ref, sem)
-    for copy in copies:
-        copy.start()
-    for side, main_ref in enumerate((down_ref, up_ref)):
-        copies[side].wait()
-
-        @pl.loop(0, RADIUS, unroll=2)
-        def _(p):
-            plane = strip_ref[side * RADIUS + p, RADIUS : cells_y - RADIUS, :]
-            main_ref[p] = (plane - 0.5).astype(BF16)
+            targets[1 + p // NEAR][p % NEAR] = plane[RADIUS : cells_y - RADIUS].astype(BF16)
+            flipped = dot(pick, plane.astype(BF16), NT)
+            pieces = [plane[:RADIUS], plane[cells_y - RADIUS :]]
+            pieces += [flipped[:, k * LANES : (k + 1) * LANES] for k in range(cells_y // LANES)]
+            pieces = jnp.concatenate(pieces, axis=0).astype(BF16)
+            targets[0][p * edge_rows : (p + 1) * edge_rows, :] = pieces
+
+
+def prefix_kernel(token_ref, out_ref):
+    out_ref[...] = onehot(iota((LANES, LANES), 0) <= iota((LANES, LANES), 1))
 
 
 def deposit_kernel(
-    cells_y, slots, design_ref, low_ref, high_ref, pay_ref, grid_ref, rows_out_ref,
-    rim_ref, own_ref, flip_ref, weight_ref, code_ref, value_ref, code_smem, value_smem, sem,
+    cells_y, slots, design_ref, low_ref, high_ref, pay_ref, prefix_ref, grid_ref, rows_out_ref,
+    small_ref, rim_ref, own_ref, flip_ref, weight_ref, code_ref, value_ref, code_smem, value_smem, sem,
 ):
     cells_x = design_ref.shape[0] // cells_y
     partners = pay_ref.shape[0]
     rim = RADIUS * cells_y
     own = cells_x * cells_y
+    edge_rows = 2 * RADIUS + RADIUS * cells_y // LANES
     copy = pltpu.make_async_copy(design_ref, grid_ref.at[pl.ds(rim, own)], sem.at[0])
     copy.start()
 
     lane = iota((1, LANES), 1)
-    upper = onehot(iota((LANES, LANES), 0) <= iota((LANES, LANES), 1))
-
-    @pl.loop(0, partners, unroll=min(partners, 16))
-    def _(p):
+    upper = prefix_ref[...]
+
+    def decode(p):
         weight_ref[pl.ds(pl.multiple_of(p * slots, 16), slots), :] = pay_ref[p, :slots, :].astype(F32)
         meta = pay_ref[p, slots : slots + 8, :].astype(F32)
         plane, line, value = meta[0:1], meta[1:2], meta[2:3]
@@ -236,46 +231,60 @@
         code_ref[pl.ds(p, 1), :] = code.astype(jnp.int32)
         value_ref[pl.ds(p, 1), :] = moved[2:3]
 
-    lists = [
-        pltpu.make_async_copy(code_ref, code_smem, sem.at[1]),
-        pltpu.make_async_copy(value_ref, value_smem, sem.at[2]),
-    ]
-    for move in lists:
-        move.start()
+    half = partners // 2
+    lists = []
+    for h in range(2):
+        part = pl.ds(h * half, half)
+        pl.loop(h * half, (h + 1) * half, unroll=min(half, 8))(decode)
+        moves = [
+            pltpu.make_async_copy(code_ref.at[part], code_smem.at[part], sem.at[1 + 2 * h]),
+            pltpu.make_async_copy(value_ref.at[part], value_smem.at[part], sem.at[2 + 2 * h]),
+        ]
+        for move in moves:
+            move.start()
+        lists.append(moves)
     zeros = jnp.zeros((cells_y, LANES), F32)
     for p in range(RADIUS):
         grid_ref[p * cells_y : (p + 1) * cells_y, :] = zeros
         grid_ref[rim + own + p * cells_y : rim + own + (p + 1) * cells_y, :] = zeros
-    for move in lists:
-        move.wait()
     copy.wait()
 
-    @pl.loop(0, partners)
-    def _(p):
-        @pl.loop(0, (code_smem[p, LANES - 1] + 3) // 4)
+    def scatter(p):
+        @pl.loop(0, (code_smem[p, LANES - 1] + GROUP - 1) // GROUP)
         def _(j):
-            for k in range(4):
-                code = code_smem[p, j * 4 + k]
-                row = code // LANES
-                amount = value_smem[p, j * 4 + k] * weight_ref[pl.ds(p * slots + code % LANES, 1), :]
-                grid_ref[pl.ds(row, 1), :] = grid_ref[pl.ds(row, 1), :] + amount
+            codes = [code_smem[p, j * GROUP + k] for k in range(GROUP)]
+            spots = [code // LANES for code in codes]
+            amounts = [
+                value_smem[p, j * GROUP + k] * weight_ref[pl.ds(p * slots + codes[k] % LANES, 1), :]
+                for k in range(GROUP)
+            ]
+            olds = [grid_ref[pl.ds(spot, 1), :] for spot in spots]
+            for k in range(GROUP):
+                amount = amounts[k]
+                for i in range(k):
+                    amount = amount + jnp.where(spots[i] == spots[k], 1.0, 0.0) * amounts[i]
+                grid_ref[pl.ds(spots[k], 1), :] = olds[k] + amount
+
+    for h in range(2):
+        for move in lists[h]:
+            move.wait()
+        pl.loop(h * half, (h + 1) * half)(scatter)
 
     total = cells_x + 2 * RADIUS
     pick = picker()
 
-    @pl.loop(0, cells_x, unroll=4)
+    @pl.loop(0, cells_x, unroll=16)
     def _(x):
         plane = clipped(grid_ref[pl.ds(rim + x * cells_y, cells_y), :] - 0.5)
         flip_ref[x + RADIUS] = dot(pick, plane.astype(BF16), NT)
 
     for source_ref, base in ((low_ref, 0), (high_ref, RADIUS + cells_x)):
-        @pl.loop(0, RADIUS, unroll=4)
-        def _(p):
+        for p in range(RADIUS):
             plane = grid_ref[pl.ds((base + p) * cells_y, cells_y), :]
             deposited = dot(pick, plane.astype(BF16), NT)
             raw = jnp.concatenate(
                 [
-                    source_ref[p, (2 + k) * RADIUS : (3 + k) * RADIUS].astype(F32)
+                    source_ref[pl.ds(p * edge_rows + (2 + k) * RADIUS, RADIUS), :].astype(F32)
                     for k in range(cells_y // LANES)
                 ],
                 axis=1,
@@ -286,7 +295,8 @@
         for p in range(RADIUS):
             for k, start in enumerate((0, cells_y - RADIUS)):
                 at = (base + p) * cells_y + start
-                edge = source_ref[p, k * RADIUS : (k + 1) * RADIUS].astype(F32)
+                edge = source_ref[p * edge_rows + k * RADIUS : p * edge_rows + (k + 1) * RADIUS, :]
+                edge = edge.astype(F32)
                 grid_ref[at : at + RADIUS, :] = grid_ref[at : at + RADIUS, :] + edge
 
     for k, start in enumerate((0, cells_y - RADIUS)):
@@ -298,32 +308,38 @@
         for i, value in enumerate(running(planes, cells_x)):
             rows_out_ref[i, k * RADIUS : (k + 1) * RADIUS, :] = value
 
+    double = 2 * RADIUS
+    rows = rows_out_ref[...].reshape(cells_x * double, LANES).astype(BF16)
+    first = jnp.where(lax.axis_index("gz") == 0, LANES - RADIUS, 0)
+    tiled = onehot(iota((LANES, LANES), 0) == iota((LANES, LANES), 1) % RADIUS + first)
+    shape = (cells_x * double, LANES)
+    mine = iota(shape, 0) % double == iota(shape, 1) // RADIUS
+    small = jnp.where(mine, dot(rows, tiled), 0.0).reshape(cells_x, double, LANES)
+    small_ref[...] = jnp.sum(small, axis=1).astype(BF16)
+
     for i, value in enumerate(running([flip_ref[e] for e in range(total)], cells_x)):
         rim_ref[i] = value.astype(BF16)
 
 
-def edge_kernel(rows_ref, rim_ref, first_ref, last_ref):
+def edge_kernel(rows_ref, small_ref, first_ref, last_ref):
     cells_x, double, cells_z = rows_ref.shape
-    cells_y = rim_ref.shape[2]
     weights = cone(iota((cells_z, cells_z), 0) - iota((cells_z, cells_z), 1))
     weights = jnp.concatenate([weights, weights], axis=0)
-    side = side_weights()
+    side = jnp.concatenate([side_weights()] * double, axis=0)
     rows = rows_ref[...].reshape(cells_x * double, cells_z)
-    value = dot(jnp.concatenate(halves(rows), axis=1), weights)
+    shape = (cells_x * double, LANES)
+    repeat = onehot(iota((shape[0], cells_x), 0) // double == iota((shape[0], cells_x), 1))
+    mine = iota(shape, 0) % double == iota(shape, 1) // RADIUS
+    spread = jnp.where(mine, dot(repeat, small_ref[...]), 0.0).astype(BF16)
+    value = dot(jnp.concatenate(halves(rows), axis=1), weights) + dot(spread, side)
+    value = value.astype(BF16)
     for x in range(cells_x):
-        for k, out_ref in enumerate((first_ref, last_ref)):
-            start = 0 if k == 0 else cells_y - LANES
-            shift = 0 if k == 0 else LANES - RADIUS
-            rim = rim_ref[x, :, start : start + LANES][:, shift : shift + RADIUS]
-            at = x * double + k * RADIUS
-            out_ref[x] = (value[at : at + RADIUS] + dot(rim, side, TN)).astype(BF16)
-
-
-STEP = 8
+        first_ref[x] = value[x * double : x * double + RADIUS]
+        last_ref[x] = value[x * double + RADIUS : (x + 1) * double]
 
 
 def project_planes(
-    scale_total, depth, places, smooth_ref, rim_ref, ends_ref, proj_ref, done
+    scale_total, depth, places, step, smooth_ref, rim_ref, ends_ref, proj_ref, done
 ):
     _, _, cells_y = rim_ref.shape
     cells_z = proj_ref.shape[1]
@@ -338,13 +354,13 @@
     scale = 8.0 / (scale_total * inside)
     top = math.tanh(4.0)
 
-    @pl.loop(0, places[1])
+    @pl.loop(0, places[1], unroll=STEP // step)
     def _(g):
         base = places[0] + g * places[2]
-        rims = rim_ref[pl.ds(base, STEP)].reshape(STEP * RADIUS, cells_y)
+        rims = rim_ref[pl.ds(base, step)].reshape(step * RADIUS, cells_y)
         rims = dot(rims, across)
-        for pair in range(STEP // 2):
-            both = [smooth_ref[g * STEP + 2 * pair + k] for k in range(2)]
+        for pair in range(step // 2):
+            both = [smooth_ref[g * step + 2 * pair + k] for k in range(2)]
             both = dot(across, jnp.concatenate(both, axis=1)).astype(BF16)
             for k in range(2):
                 x = base + 2 * pair + k
@@ -361,8 +377,30 @@
         done(g)
 
 
+def smooth_x(grid_ref, pad_ref, low, high, start, rows, main):
+    cells_y = pad_ref.shape[1]
+    cells_x = grid_ref.shape[0] // cells_y - 2 * RADIUS
+
+    def plane(e):
+        at = pl.multiple_of(e * cells_y + start, rows)
+        value = grid_ref[pl.ds(at, rows), :]
+        if RADIUS <= e < RADIUS + cells_x:
+            return clipped(value - 0.5)
+        p = e if e < RADIUS else e - cells_x
+        rim = pad_ref[p, pl.ds(start, rows), :].astype(F32)
+        return clipped(value + jnp.where(main, rim, 0.0))
+
+    return running([plane(e) for e in range(low, high + 2 * RADIUS)], high - low)
+
+
+def main_rows(start, rows, cells_y):
+    row = start + iota((rows, 1), 0)
+    return (row >= RADIUS) & (row < cells_y - RADIUS)
+
+
 def inner_kernel(
-    scale_total, depth, grid_ref, rim_ref, before_ref, after_ref, proj_ref, ends_ref, smooth_ref
+    scale_total, depth, grid_ref, low_ref, high_ref, rim_ref, before_ref, after_ref, proj_ref,
+    ends_ref, pad_ref, smooth_ref,
 ):
     cells_x, _, cells_y = rim_ref.shape
     cells_z = proj_ref.shape[1]
@@ -373,28 +411,30 @@
     for rows_in_ref, distance, index in ((before_ref, gap + RADIUS, 0), (after_ref, gap - RADIUS, 1)):
         weights = jnp.where(same, cone(distance).astype(F32), 0.0).astype(BF16)
         ends_ref[index] = dot(weights, rows_in_ref[...].reshape(many, cells_z))
-    count = cells_x - 2 * RADIUS
+    count = cells_x - RADIUS
     chunk = 16
+    for p in range(NEAR):
+        pad_ref[NEAR + p, RADIUS : cells_y - RADIUS, :] = low_ref[p]
+        pad_ref[RADIUS + p, RADIUS : cells_y - RADIUS, :] = high_ref[p]
 
     @pl.loop(0, cells_y // chunk)
     def _(j):
         start = pl.multiple_of(j * chunk, chunk)
-        planes = []
-        for e in range(RADIUS, RADIUS + cells_x):
-            at = pl.multiple_of(e * cells_y + start, chunk)
-            planes.append(clipped(grid_ref[pl.ds(at, chunk), :] - 0.5))
-        for i, value in enumerate(running(planes, count)):
+        main = main_rows(start, chunk, cells_y)
+        values = smooth_x(grid_ref, pad_ref, NEAR, cells_x - NEAR, start, chunk, main)
+        for i, value in enumerate(values):
             smooth_ref[i, pl.ds(start, chunk), :] = value.astype(BF16)
 
     project_planes(
-        scale_total, depth, (RADIUS, count // STEP, STEP), smooth_ref, rim_ref, ends_ref,
+        scale_total, depth, (NEAR, count // STEP, STEP), STEP, smooth_ref, rim_ref, ends_ref,
         proj_ref, lambda g: None,
     )
 
 
 def finish_kernel(
-    scale_total, depth, inner_ref, own_ref, grid_ref, low_ref, high_ref, rim_ref, ends_ref,
-    pay_ref, proj_ref, out_ref, ratio_ref, pad_ref, smooth_ref, picked_ref, rows_ref, sem, own_sem,
+    scale_total, depth, inner_ref, own_ref, grid_ref, low_near_ref, high_near_ref, low_far_ref,
+    high_far_ref, rim_ref, ends_ref, pay_ref, proj_ref, out_ref, ratio_ref, pad_ref, smooth_ref,
+    picked_ref, rows_ref, sem, own_sem,
 ):
     cells_x, _, cells_y = rim_ref.shape
     cells_z = out_ref.shape[1]
@@ -408,39 +448,26 @@
         rows = pl.ds(pl.multiple_of(first * cells_y, 8), count * cells_y)
         return pltpu.make_async_copy(proj_ref.at[rows], out_ref.at[rows], sem.at[index])
 
-    inner_send = send(RADIUS, cells_x - 2 * RADIUS, 2)
+    inner_send = send(NEAR, cells_x - RADIUS, 2)
     inner_send.start()
-    for p in range(RADIUS):
-        pad_ref[p, RADIUS : cells_y - RADIUS, :] = low_ref[p]
-        pad_ref[RADIUS + p, RADIUS : cells_y - RADIUS, :] = high_ref[p]
+    sources = (low_far_ref, low_near_ref, high_near_ref, high_far_ref)
+    for index, source_ref in enumerate(sources):
+        for p in range(NEAR):
+            pad_ref[index * NEAR + p, RADIUS : cells_y - RADIUS, :] = source_ref[p]
 
     @pl.loop(0, cells_y // chunk)
     def _(j):
         start = pl.multiple_of(j * chunk, chunk)
-        row = start + iota((chunk, 1), 0)
-        main = (row >= RADIUS) & (row < cells_y - RADIUS)
-
-        def own(e):
-            at = pl.multiple_of(e * cells_y + start, chunk)
-            return clipped(grid_ref[pl.ds(at, chunk), :] - 0.5)
-
-        def outer(e, p):
-            at = pl.multiple_of(e * cells_y + start, chunk)
-            rim = pad_ref[p, pl.ds(start, chunk), :].astype(F32)
-            return clipped(grid_ref[pl.ds(at, chunk), :] + jnp.where(main, rim, 0.0))
-
-        planes = [outer(e, e) for e in range(RADIUS)]
-        planes += [own(e) for e in range(RADIUS, 3 * RADIUS)]
-        for i, value in enumerate(running(planes, RADIUS)):
+        main = main_rows(start, chunk, cells_y)
+        values = smooth_x(grid_ref, pad_ref, 0, NEAR, start, chunk, main)
+        values += smooth_x(grid_ref, pad_ref, cells_x - NEAR, cells_x, start, chunk, main)
+        for i, value in enumerate(values):
             smooth_ref[i, pl.ds(start, chunk), :] = value.astype(BF16)
-        planes = [own(e) for e in range(cells_x - RADIUS, cells_x + RADIUS)]
-        planes += [outer(cells_x + RADIUS + p, RADIUS + p) for p in range(RADIUS)]
-        for i, value in enumerate(running(planes, RADIUS)):
-            smooth_ref[RADIUS + i, pl.ds(start, chunk), :] = value.astype(BF16)
-
+
+    last = cells_x - NEAR
     project_planes(
-        scale_total, depth, (0, 2, cells_x - RADIUS), smooth_ref, rim_ref, ends_ref, proj_ref,
-        lambda g: send(g * (cells_x - RADIUS), RADIUS, g).start(),
+        scale_total, depth, (0, 2, last), NEAR, smooth_ref, rim_ref, ends_ref, proj_ref,
+        lambda g: send(g * last, NEAR, g).start(),
     )
     fetch.wait()
 
@@ -462,7 +489,7 @@
         ratio_ref[pl.ds(c, 1), :] = (amount / dot(ones, w, NT))[:1]
 
     for g in range(2):
-        send(g * (cells_x - RADIUS), RADIUS, g).wait()
+        send(g * last, NEAR, g).wait()
     inner_send.wait()
 
 
@@ -527,7 +554,10 @@
 
     inner = cells_y - 2 * RADIUS
     edge_rows = 2 * RADIUS + RADIUS * cells_y // LANES
-    payload = pl.pallas_call(
+    up = [(i, (i + 1) % n_tx) for i in range(n_tx)]
+    down = [(t, s) for s, t in up]
+
+    call = pl.pallas_call(
         functools.partial(pack_kernel, n_ty, cells_x, cells_y),
         out_shape=shape((tiles, slots + 8, LANES), BF16),
         in_specs=[anywhere] * 8,
@@ -546,7 +576,8 @@
         ],
         compiler_params=params(24),
         name="pack",
-    )(
+    )
+    operands = (
         stay(slot_counts),
         stay(quad_weights),
         stay(edge_basis.T),
@@ -556,42 +587,52 @@
         stay(slot_elements),
         stay(slot_blocks),
     )
+    payload = call(*operands)
 
     arrived = lax.all_to_all(payload, ("tx", "ty"), split_axis=0, concat_axis=0, tiled=True)
-    up = [(i, (i + 1) % n_tx) for i in range(n_tx)]
-    down = [(t, s) for s, t in up]
-
-    def cast(kernel, rows, token):
-        strip = shape((RADIUS, rows, LANES), BF16)
-        return pl.pallas_call(
-            kernel,
-            out_shape=(strip, strip),
-            in_specs=[anywhere, anywhere],
-            out_specs=(whole, whole),
-            scratch_shapes=[
-                VMEM((2 * RADIUS, cells_y, cells_z), F32),
-                pltpu.SemaphoreType.DMA((2,)),
-            ],
-            compiler_params=params(16),
-        )(stay(design), token)
-
-    up_edge, down_edge = cast(cast_edge_kernel, edge_rows, stay(payload))
-    low_edge = lax.ppermute(up_edge, "tx", up)
-    high_edge = lax.ppermute(down_edge, "tx", down)
-    up_main, down_main = cast(cast_main_kernel, inner, up_edge)
-    low_main = lax.ppermute(up_main, "tx", up)
-    high_main = lax.ppermute(down_main, "tx", down)
-
-    grid, edge_smooth, rim, rows_own = pl.pallas_call(
+    strip = shape((NEAR, inner, LANES), BF16)
+    rim_edge = shape((RADIUS * edge_rows, LANES), BF16)
+    call = pl.pallas_call(
+        cast_kernel,
+        out_shape=(rim_edge,) * 2 + (strip,) * 4,
+        in_specs=[anywhere] * 2,
+        out_specs=(whole,) * 6,
+        scratch_shapes=[
+            VMEM((2 * RADIUS, cells_y, cells_z), F32),
+            pltpu.SemaphoreType.DMA((2,)),
+        ],
+        compiler_params=params(16),
+        name="cast_rims",
+    )
+    up_first, down_first, *mains = call(stay(design), stay(payload))
+    low_first = lax.ppermute(up_first, "tx", up)
+    high_first = lax.ppermute(down_first, "tx", down)
+
+    call = pl.pallas_call(
+        prefix_kernel,
+        out_shape=shape((LANES, LANES), BF16),
+        in_specs=[anywhere],
+        out_specs=whole,
+        compiler_params=params(16),
+        name="prefix",
+    )
+    prefix = call(up_first)
+    low_near = lax.ppermute(mains[0], "tx", up)
+    high_near = lax.ppermute(mains[1], "tx", down)
+    low_far = lax.ppermute(mains[2], "tx", up)
+    high_far = lax.ppermute(mains[3], "tx", down)
+
+    grid, edge_smooth, small, rim, rows_own = pl.pallas_call(
         functools.partial(deposit_kernel, cells_y, slots),
         out_shape=(
             shape((rows_ext, cells_z), F32),
             shape((cells_x, 2 * RADIUS, cells_z), F32),
+            shape((cells_x, LANES), BF16),
             shape((cells_x, RADIUS, cells_y), BF16),
             shape((tiles, LANES), jnp.int32),
         ),
-        in_specs=[anywhere] + [whole] * 3,
-        out_specs=(whole,) * 4,
+        in_specs=[anywhere] + [whole] * 4,
+        out_specs=(whole,) * 5,
         scratch_shapes=[
             VMEM((cells_x + 2 * RADIUS, RADIUS, cells_y), F32),
             VMEM((tiles * slots, LANES), F32),
@@ -599,22 +640,24 @@
             VMEM((tiles, LANES), F32),
             SMEM((tiles, LANES), jnp.int32),
             SMEM((tiles, LANES), F32),
-            pltpu.SemaphoreType.DMA((3,)),
+            pltpu.SemaphoreType.DMA((5,)),
         ],
         compiler_params=params(16),
         name="deposit",
-    )(stay(design.reshape(cells_x * cells_y, cells_z)), low_edge, high_edge, arrived)
-
+    )(stay(design.reshape(cells_x * cells_y, cells_z)), low_first, high_first, arrived, prefix)
+
+    small = lax.ppermute(small, "gz", [(0, 1), (1, 0)])
     rim = lax.ppermute(rim, "gz", [(0, 1), (1, 0)])
     edge = shape((cells_x, RADIUS, cells_z), BF16)
-    first, last = pl.pallas_call(
+    call = pl.pallas_call(
         edge_kernel,
         out_shape=(edge, edge),
         in_specs=[whole, whole],
         out_specs=(whole, whole),
         compiler_params=params(16),
         name="edges",
-    )(edge_smooth, rim)
+    )
+    first, last = call(edge_smooth, small)
     up = [(i, (i + 1) % n_ty) for i in range(n_ty)]
     down = [(t, s) for s, t in up]
     before = lax.ppermute(last, "ty", up)
@@ -625,21 +668,24 @@
     call = pl.pallas_call(
         functools.partial(inner_kernel, *constants),
         out_shape=(flat, shape((2, cells_x * RADIUS, cells_z), F32)),
-        in_specs=[whole] * 4,
+        in_specs=[whole] * 6,
         out_specs=(whole, whole),
-        scratch_shapes=[VMEM((cells_x - 2 * RADIUS, cells_y, cells_z), BF16)],
+        scratch_shapes=[
+            VMEM((2 * RADIUS, cells_y, cells_z), BF16),
+            VMEM((cells_x - RADIUS, cells_y, cells_z), BF16),
+        ],
         compiler_params=params(16),
         name="inner",
     )
-    partial, ends = call(grid, rim, before, after)
+    partial, ends = call(grid, low_near, high_near, rim, before, after)
     _, projected, ratios = pl.pallas_call(
         functools.partial(finish_kernel, *constants),
         out_shape=(flat, flat, shape((tiles * capacity // LANES, LANES), F32)),
-        in_specs=[whole] * 8,
+        in_specs=[whole] * 10,
         out_specs=(whole, anywhere, whole),
         scratch_shapes=[
             VMEM((2 * RADIUS, cells_y, cells_z), BF16),
-            VMEM((2 * RADIUS, cells_y, cells_z), BF16),
+            VMEM((RADIUS, cells_y, cells_z), BF16),
             VMEM((tiles * capacity, cells_z), F32),
             SMEM((tiles, LANES), jnp.int32),
             pltpu.SemaphoreType.DMA((3,)),
@@ -648,7 +694,9 @@
         input_output_aliases={0: 0},
         compiler_params=params(16),
         name="finish",
-    )(partial, rows_own, grid, low_main, high_main, rim, ends, arrived)
+    )(
+        partial, rows_own, grid, low_near, high_near, low_far, high_far, rim, ends, arrived
+    )
 
     ratios = ratios.reshape(tiles, capacity)
     ratios = lax.all_to_all(ratios, ("tx", "ty"), split_axis=0, concat_axis=0, tiled=True)

time: 79.8 us -> 78.4 us (0.982)
  starting transfers between devices: 16.6 us -> 28.7 us
  waiting for transfers between devices: 28.5 us -> 18.2 us
  Pallas kernels: 23 us -> 20.4 us
    ppermute x4 -> x7, starting transfers between devices: 5.9 us -> 18.3 us  [the longest x1 7.36 us: update(): low_first = lax.ppermute(up_first, 'tx', up)]
    ppermute x4 -> x7, waiting for transfers between devices: 23 us -> 16.2 us  [the longest x1 8.43 us: update(): high_first = lax.ppermute(down_first, 'tx', down)]
    ppermute x1, waiting for transfers between devices: 3.55 us -> 0.01 us  [update(): rim = lax.ppermute(rim, 'gz', [(0, 1), (1, 0)])]
    pallas_call x1, Pallas kernels: 4.57 us -> 3.07 us  [update(): pl.pallas_call(functools.partial(finish_kernel, *constants), out_shape=(f...]
  transfers between devices with their start and end apart: 8 -> 11, of which waited for: 4 -> 4; matrix products, arithmetic and copies ran while one was open for 0% -> 0% of each run, Pallas kernels for 18% -> 17%
where the time goes in v2:
time: 78.4 us; the launch traced here: 78 us
  starting transfers between devices  28.7 us (37%)
  Pallas kernels  20.4 us (26%)
  waiting for transfers between devices  18.2 us (23%)
  blocking collectives  9.89 us (13%)
    all_to_all x1, blocking collectives, update(): lax.all_to_all(ratios, ('tx', 'ty'), split_axis=0, concat_axis=0, tiled=T...  9.89 us
    ppermute x1, waiting for transfers between devices, update(): high_first = lax.ppermute(down_first, 'tx', down)  8.43 us
    all_to_all x1, starting transfers between devices, update(): lax.all_to_all(payload, ('tx', 'ty'), split_axis=0, concat_axis=0, tiled=...  7.43 us
    ppermute x1, starting transfers between devices, update(): low_first = lax.ppermute(up_first, 'tx', up)  7.36 us
    pallas_call x1, Pallas kernels, update(): pl.pallas_call(functools.partial(deposit_kernel, cells_y, slots), out_sha...  6.61 us
    ppermute x1, waiting for transfers between devices, update(): low_first = lax.ppermute(up_first, 'tx', up)  5.34 us
    pallas_call x1, Pallas kernels, update(): partial, ends = call(grid, low_near, high_near, rim, before, after)  4.77 us
    ppermute x1, starting transfers between devices, update(): high_far = lax.ppermute(mains[3], 'tx', down)  3.72 us
  transfers between devices with their start and end apart: 11, of which 4 were waited for; matrix products, arithmetic and copies ran while one was open for 0% of the time, Pallas kernels for 17%

profile of v2, /device:TPU:0, one launch (start us, length us, event | category | flops | bytes accessed | tf_op | source)
XLA Modules:
  0.0 78.0 jit_solution(7168502532875947213)
XLA Ops:
  0.6 2.8 %pack.1.token_ref = bf16[16,56,128]{2,1,0:T(8,128)(2,1)} custom-call(s32[1,16]{1,0:T(1,128)} %counts_ref.1, f32[8]{0:T(128)} %quad_hbm.1, f32[12,24]{1,0:T(8,128)} %bitcast.13, f32[12,2,2048]{2,1,0:T(2,128)} %bitcast.10, f32[12,2,2048]{2,1,0:T(2,128)} %bitcast.11, bf16[16,16,128]{2,1,0:T(8,128)(2,1)} %weights_hbm.1, s32[16,16]{1,0:T(8,128)} %elements_ref.1, ...), custom_call_target="tpu_custom_call" | custom-call | tf_op jit(solution)/shard_map/pack/pallas_call | solution.py:590
  3.5 7.4 %all-to-all-start = ((bf16[16,56,128]{2,1,0:T(8,128)(2,1)}), bf16[16,56,128]{2,1,0:T(8,128)(2,1)S(1)}, u32[]{:S(2)}, u32[]{:S(2)}) async-start(bf16[16,56,128]{2,1,0:T(8,128)(2,1)} %pack.1.token_ref), calls=%async_computation | async-start | bytes 458752 | tf_op jit(solution)/shard_map/all_to_all | solution.py:592
  10.9 1.8 %cast_rims.1 = (bf16[256,128]{1,0:T(8,128)(2,1)S(1)}, bf16[256,128]{1,0:T(8,128)(2,1)S(1)}, bf16[4,240,128]{2,1,0:T(8,128)(2,1)S(1)}, bf16[4,240,128]{2,1,0:T(8,...) custom-call(f32[32,256,128]{2,1,0:T(8,128)} %design_ref.1, ...), custom_call_target="tpu_custom_call" | custom-call | tf_op jit(solution)/shard_map/cast_rims/pallas_call | solution.py:607
  12.7 2.0 %collective-permute-start.2 = (bf16[4,240,128]{2,1,0:T(8,128)(2,1)S(1)}, bf16[4,240,128]{2,1,0:T(8,128)(2,1)S(1)}, u32[]{:S(2)}, u32[]{:S(2)}) collective-permute-start(bf16[4,240,128]{2,1,0:T(8,128)(2,1)S(1)} %get-tuple-element.22), channel_id=1, source_target_pairs={{0,8},{8,16},{16,24},{24,0},{1,9},{9,17},{17,25},{25,1},{2,10},{10... | collective-permute-start | bytes 737288 | tf_op jit(solution)/shard_map/ppermute | solution.py:620
  14.7 1.9 %collective-permute-start.3 = (bf16[4,240,128]{2,1,0:T(8,128)(2,1)S(1)}, bf16[4,240,128]{2,1,0:T(8,128)(2,1)S(1)}, u32[]{:S(2)}, u32[]{:S(2)}) collective-permute-start(bf16[4,240,128]{2,1,0:T(8,128)(2,1)S(1)} %get-tuple-element.23), channel_id=1, source_target_pairs={{8,0},{16,8},{24,16},{0,24},{9,1},{17,9},{25,17},{1,25},{10,2},{18... | collective-permute-start | bytes 737288 | tf_op jit(solution)/shard_map/ppermute | solution.py:621
  16.6 1.9 %collective-permute-start.1 = (bf16[256,128]{1,0:T(8,128)(2,1)S(1)}, bf16[256,128]{1,0:T(8,128)(2,1)S(1)}, u32[]{:S(2)}, u32[]{:S(2)}) collective-permute-start(bf16[256,128]{1,0:T(8,128)(2,1)S(1)} %get-tuple-element.20), channel_id=1, source_target_pairs={{8,0},{16,8},{24,16},{0,24},{9,1},{17,9},{25,17},{1,25},{10,2},{18... | collective-permute-start | bytes 196616 | tf_op jit(solution)/shard_map/ppermute | solution.py:609
  18.5 0.1 collective-permute-start.8
  18.6 3.7 %collective-permute-start.9 = (bf16[4,240,128]{2,1,0:T(8,128)(2,1)S(1)}, bf16[4,240,128]{2,1,0:T(8,128)(2,1)S(1)}, u32[]{:S(2)}, u32[]{:S(2)}) collective-permute-start(bf16[4,240,128]{2,1,0:T(8,128)(2,1)S(1)} %get-tuple-element.32), channel_id=1, source_target_pairs={{8,0},{16,8},{24,16},{0,24},{9,1},{17,9},{25,17},{1,25},{10,2},{18... | collective-permute-start | bytes 737288 | tf_op jit(solution)/shard_map/ppermute | solution.py:623
  22.4 8.4 %collective-permute-done.1.high_ref = bf16[256,128]{1,0:T(8,128)(2,1)S(1)} collective-permute-done((bf16[256,128]{1,0:T(8,128)(2,1)S(1)}, bf16[256,128]{1,0:T(8,128)(2,1)S(1)}, u32[]{:S(2)}, u32[]{:S(2)}) %collective-permute-start.1) | collective-permute-done | bytes 65568 | tf_op jit(solution)/shard_map/ppermute | solution.py:609
  30.8 7.4 %collective-permute-start = (bf16[256,128]{1,0:T(8,128)(2,1)S(1)}, bf16[256,128]{1,0:T(8,128)(2,1)S(1)}, u32[]{:S(2)}, u32[]{:S(2)}) collective-permute-start(bf16[256,128]{1,0:T(8,128)(2,1)S(1)} %get-tuple-element.19.token_ref), channel_id=1, source_target_pairs={{0,8},{8,16},{16,24},{24,0},{1,9},{9,17},{17,25},{25,1},{2,10},{10... | collective-permute-start | bytes 196616 | tf_op jit(solution)/shard_map/ppermute | solution.py:608
  38.2 5.3 %collective-permute-done.low_ref = bf16[256,128]{1,0:T(8,128)(2,1)S(1)} collective-permute-done((bf16[256,128]{1,0:T(8,128)(2,1)S(1)}, bf16[256,128]{1,0:T(8,128)(2,1)S(1)}, u32[]{:S(2)}, u32[]{:S(2)}) %collective-permute-start) | collective-permute-done | bytes 65568 | tf_op jit(solution)/shard_map/ppermute | solution.py:608
  43.5 0.0 all-to-all-done.pay_ref
  43.5 6.6 %deposit.1 = (f32[12288,128]{1,0:T(8,128)S(1)}, f32[32,16,128]{2,1,0:T(8,128)S(1)}, bf16[32,128]{1,0:T(8,128)(2,1)S(1)}, bf16[32,8,256]{2,1,0:T(8,128)(2,1)S(1)}, s32[16,128]{1,0:T(8,128)S(1)}) custom-call(f32[8192,128]{1,0:T(8,128)} %bitcast.9, bf16[256,128]{1,0:T(8,128)(2,1)S(1)} %collective-permute-done.low_ref, ...), custom_call_target="tpu_custom_call" | custom-call | tf_op jit(solution)/shard_map/deposit/pallas_call | solution.py:625
  50.1 1.3 %collective-permute-start.5 = (bf16[32,128]{1,0:T(8,128)(2,1)S(1)}, bf16[32,128]{1,0:T(8,128)(2,1)S(1)}, u32[]{:S(2)}, u32[]{:S(2)}) collective-permute-start(bf16[32,128]{1,0:T(8,128)(2,1)S(1)} %get-tuple-element.26), channel_id=1, source_target_pairs={{0,1},{1,0},{2,3},{3,2},{4,5},{5,4},{6,7},{7,6},{8,9},{9,8},{10,11... | collective-permute-start | bytes 24584 | tf_op jit(solution)/shard_map/ppermute | solution.py:649
  51.4 2.4 %collective-permute-done.5.small_ref = bf16[32,128]{1,0:T(8,128)(2,1)S(1)} collective-permute-done((bf16[32,128]{1,0:T(8,128)(2,1)S(1)}, bf16[32,128]{1,0:T(8,128)(2,1)S(1)}, u32[]{:S(2)}, u32[]{:S(2)}) %collective-permute-start.5) | collective-permute-done | bytes 8224 | tf_op jit(solution)/shard_map/ppermute | solution.py:649
  53.9 1.2 %collective-permute-start.4 = (bf16[32,8,256]{2,1,0:T(8,128)(2,1)S(1)}, bf16[32,8,256]{2,1,0:T(8,128)(2,1)S(1)}, u32[]{:S(2)}, u32[]{:S(2)}) collective-permute-start(bf16[32,8,256]{2,1,0:T(8,128)(2,1)S(1)} %get-tuple-element.24), channel_id=1, source_target_pairs={{0,1},{1,0},{2,3},{3,2},{4,5},{5,4},{6,7},{7,6},{8,9},{9,8},{10,11... | collective-permute-start | bytes 393224 | tf_op jit(solution)/shard_map/ppermute | solution.py:650
  55.1 0.4 edges.1
  55.4 0.0 collective-permute-done.2.low_ref.low_near_ref
  55.5 0.1 collective-permute-start.6
  55.5 0.0 collective-permute-done.3.high_ref.high_near_ref
  55.5 1.7 %collective-permute-start.7 = (bf16[32,8,128]{2,1,0:T(8,128)(2,1)S(1)}, bf16[32,8,128]{2,1,0:T(8,128)(2,1)S(1)}, u32[]{:S(2)}, u32[]{:S(2)}) collective-permute-start(bf16[32,8,128]{2,1,0:T(8,128)(2,1)S(1)} %get-tuple-element.28), channel_id=1, source_target_pairs={{2,0},{4,2},{6,4},{0,6},{3,1},{5,3},{7,5},{1,7},{10,8},{12,10},{14... | collective-permute-start | bytes 196616 | tf_op jit(solution)/shard_map/ppermute | solution.py:664
  57.3 1.9 %collective-permute-done.6.before_ref = bf16[32,8,128]{2,1,0:T(8,128)(2,1)S(1)} collective-permute-done((bf16[32,8,128]{2,1,0:T(8,128)(2,1)S(1)}, bf16[32,8,128]{2,1,0:T(8,128)(2,1)S(1)}, u32[]{:S(2)}, u32[]{:S(2)}) %collective-permute-start.6) | collective-permute-done | bytes 65568 | tf_op jit(solution)/shard_map/ppermute | solution.py:663
  59.2 0.0 collective-permute-done.7.after_ref
  59.2 0.0 collective-permute-done.4.rim_ref
  59.2 4.8 %inner.1 = (f32[8192,128]{1,0:T(8,128)S(1)}, f32[2,256,128]{2,1,0:T(8,128)S(1)}) custom-call(f32[12288,128]{1,0:T(8,128)S(1)} %get-tuple-element.21.grid_ref, bf16[4,240,128]{2,1,0:T(8,128)(2,1)S(1)} %collective-permute-done.2.low_ref.low_near_ref, bf16[4,240,128]{2,1,0:T(8,128)(2,1)S(1)} %collective-permute-done.3.high_ref.high_near_ref, ...), custom_call_target="tpu_custom_call" | custom-call | tf_op jit(solution)/shard_map/inner/pallas_call | solution.py:680
  64.0 0.0 collective-permute-done.8.low_far_ref
  64.0 0.0 collective-permute-done.9.high_far_ref
  64.0 0.0 copy-start
  64.0 0.0 copy-start.1
  64.0 3.1 %finish.1 = (f32[8192,128]{1,0:T(8,128)S(1)}, f32[8192,128]{1,0:T(8,128)}, f32[2,128]{1,0:T(2,128)S(1)}) custom-call(f32[8192,128]{1,0:T(8,128)S(1)} %get-tuple-element.29.inner_ref, s32[16,128]{1,0:T(8,128)S(1)} %get-tuple-element.30.own_ref, f32[12288,128]{1,0:T(8,128)S(1)} %get-tuple-element.21.grid_ref, ...), custom_call_target="tpu_custom_call", output_to_operand_aliasing={{0}: (0, {})} | custom-call | tf_op jit(solution)/shard_map/finish/pallas_call | solution.py:681
  67.1 0.1 all_to_all.11
  67.2 9.9 %all_to_all.16 = f32[16,1,16]{2,1,0:T(1,128)S(1)} all-to-all(f32[16,1,16]{2,1,0:T(1,128)S(1)} %bitcast.12), channel_id=1, replica_groups=mesh['tx'=4,'ty'=4,'gz'=2] {'tx','ty'}, dimensions={0} | all-to-all | bytes 2048 | tf_op jit(solution)/shard_map/all_to_all | solution.py:702
  77.1 0.0 copy-done
  77.1 0.0 copy-done.1
  77.1 1.0 %to_elements.1 = f32[16,128]{1,0:T(8,128)} custom-call(s32[1,16]{1,0:T(1,128)S(1)} %copy-done.1, s32[16,16]{1,0:T(8,128)S(1)} %copy-done, f32[16,16]{1,0:T(8,128)S(1)} %bitcast.8), custom_call_target="tpu_custom_call" | custom-call | tf_op jit(solution)/shard_map/to_elements/pallas_call | solution.py:703
  (1 shorter events, 0.0 us)
Async XLA Ops:
  3.5 40.0 %all-to-all-start = ((bf16[16,56,128]{2,1,0:T(8,128)(2,1)}), bf16[16,56,128]{2,1,0:T(8,128)(2,1)S(1)}, u32[]{:S(2)}, u32[]{:S(2)}) async-start(bf16[16,56,128]{2,1,0:T(8,128)(2,1)} %pack.1.token_ref), calls=%async_computation | async-start | bytes 458752 | tf_op jit(solution)/shard_map/all_to_all | solution.py:592
  12.7 42.7 %collective-permute-start.2 = (bf16[4,240,128]{2,1,0:T(8,128)(2,1)S(1)}, bf16[4,240,128]{2,1,0:T(8,128)(2,1)S(1)}, u32[]{:S(2)}, u32[]{:S(2)}) collective-permute-start(bf16[4,240,128]{2,1,0:T(8,128)(2,1)S(1)} %get-tuple-element.22), channel_id=1, source_target_pairs={{0,8},{8,16},{16,24},{24,0},{1,9},{9,17},{17,25},{25,1},{2,10},{10... | collective-permute-start | bytes 737288 | tf_op jit(solution)/shard_map/ppermute | solution.py:620
  14.7 40.8 %collective-permute-start.3 = (bf16[4,240,128]{2,1,0:T(8,128)(2,1)S(1)}, bf16[4,240,128]{2,1,0:T(8,128)(2,1)S(1)}, u32[]{:S(2)}, u32[]{:S(2)}) collective-permute-start(bf16[4,240,128]{2,1,0:T(8,128)(2,1)S(1)} %get-tuple-element.23), channel_id=1, source_target_pairs={{8,0},{16,8},{24,16},{0,24},{9,1},{17,9},{25,17},{1,25},{10,2},{18... | collective-permute-start | bytes 737288 | tf_op jit(solution)/shard_map/ppermute | solution.py:621
  16.6 14.2 %collective-permute-start.1 = (bf16[256,128]{1,0:T(8,128)(2,1)S(1)}, bf16[256,128]{1,0:T(8,128)(2,1)S(1)}, u32[]{:S(2)}, u32[]{:S(2)}) collective-permute-start(bf16[256,128]{1,0:T(8,128)(2,1)S(1)} %get-tuple-element.20), channel_id=1, source_target_pairs={{8,0},{16,8},{24,16},{0,24},{9,1},{17,9},{25,17},{1,25},{10,2},{18... | collective-permute-start | bytes 196616 | tf_op jit(solution)/shard_map/ppermute | solution.py:609
  18.5 45.4 %collective-permute-start.8 = (bf16[4,240,128]{2,1,0:T(8,128)(2,1)S(1)}, bf16[4,240,128]{2,1,0:T(8,128)(2,1)S(1)}, u32[]{:S(2)}, u32[]{:S(2)}) collective-permute-start(bf16[4,240,128]{2,1,0:T(8,128)(2,1)S(1)} %get-tuple-element.31), channel_id=1, source_target_pairs={{0,8},{8,16},{16,24},{24,0},{1,9},{9,17},{17,25},{25,1},{2,10},{10... | collective-permute-start | bytes 737288 | tf_op jit(solution)/shard_map/ppermute | solution.py:622
  18.6 45.3 %collective-permute-start.9 = (bf16[4,240,128]{2,1,0:T(8,128)(2,1)S(1)}, bf16[4,240,128]{2,1,0:T(8,128)(2,1)S(1)}, u32[]{:S(2)}, u32[]{:S(2)}) collective-permute-start(bf16[4,240,128]{2,1,0:T(8,128)(2,1)S(1)} %get-tuple-element.32), channel_id=1, source_target_pairs={{8,0},{16,8},{24,16},{0,24},{9,1},{17,9},{25,17},{1,25},{10,2},{18... | collective-permute-start | bytes 737288 | tf_op jit(solution)/shard_map/ppermute | solution.py:623
  30.8 12.7 %collective-permute-start = (bf16[256,128]{1,0:T(8,128)(2,1)S(1)}, bf16[256,128]{1,0:T(8,128)(2,1)S(1)}, u32[]{:S(2)}, u32[]{:S(2)}) collective-permute-start(bf16[256,128]{1,0:T(8,128)(2,1)S(1)} %get-tuple-element.19.token_ref), channel_id=1, source_target_pairs={{0,8},{8,16},{16,24},{24,0},{1,9},{9,17},{17,25},{25,1},{2,10},{10... | collective-permute-start | bytes 196616 | tf_op jit(solution)/shard_map/ppermute | solution.py:608
  50.1 3.7 %collective-permute-start.5 = (bf16[32,128]{1,0:T(8,128)(2,1)S(1)}, bf16[32,128]{1,0:T(8,128)(2,1)S(1)}, u32[]{:S(2)}, u32[]{:S(2)}) collective-permute-start(bf16[32,128]{1,0:T(8,128)(2,1)S(1)} %get-tuple-element.26), channel_id=1, source_target_pairs={{0,1},{1,0},{2,3},{3,2},{4,5},{5,4},{6,7},{7,6},{8,9},{9,8},{10,11... | collective-permute-start | bytes 24584 | tf_op jit(solution)/shard_map/ppermute | solution.py:649
  53.9 5.3 %collective-permute-start.4 = (bf16[32,8,256]{2,1,0:T(8,128)(2,1)S(1)}, bf16[32,8,256]{2,1,0:T(8,128)(2,1)S(1)}, u32[]{:S(2)}, u32[]{:S(2)}) collective-permute-start(bf16[32,8,256]{2,1,0:T(8,128)(2,1)S(1)} %get-tuple-element.24), channel_id=1, source_target_pairs={{0,1},{1,0},{2,3},{3,2},{4,5},{5,4},{6,7},{7,6},{8,9},{9,8},{10,11... | collective-permute-start | bytes 393224 | tf_op jit(solution)/shard_map/ppermute | solution.py:650
  55.5 3.7 %collective-permute-start.6 = (bf16[32,8,128]{2,1,0:T(8,128)(2,1)S(1)}, bf16[32,8,128]{2,1,0:T(8,128)(2,1)S(1)}, u32[]{:S(2)}, u32[]{:S(2)}) collective-permute-start(bf16[32,8,128]{2,1,0:T(8,128)(2,1)S(1)} %get-tuple-element.27), channel_id=1, source_target_pairs={{0,2},{2,4},{4,6},{6,0},{1,3},{3,5},{5,7},{7,1},{8,10},{10,12},{12... | collective-permute-start | bytes 196616 | tf_op jit(solution)/shard_map/ppermute | solution.py:663
  55.5 3.7 %collective-permute-start.7 = (bf16[32,8,128]{2,1,0:T(8,128)(2,1)S(1)}, bf16[32,8,128]{2,1,0:T(8,128)(2,1)S(1)}, u32[]{:S(2)}, u32[]{:S(2)}) collective-permute-start(bf16[32,8,128]{2,1,0:T(8,128)(2,1)S(1)} %get-tuple-element.28), channel_id=1, source_target_pairs={{2,0},{4,2},{6,4},{0,6},{3,1},{5,3},{7,5},{1,7},{10,8},{12,10},{14... | collective-permute-start | bytes 196616 | tf_op jit(solution)/shard_map/ppermute | solution.py:664
  64.0 13.1 %copy-start = (s32[16,16]{1,0:T(8,128)S(1)}, s32[16,16]{1,0:T(8,128)}, u32[]{:S(2)}) copy-start(s32[16,16]{1,0:T(8,128)} %elements_ref.1) | copy-start | bytes 3076
  64.0 13.1 %copy-start.1 = (s32[1,16]{1,0:T(1,128)S(1)}, s32[1,16]{1,0:T(1,128)}, u32[]{:S(2)}) copy-start(s32[1,16]{1,0:T(1,128)} %counts_ref.1) | copy-start | bytes 196

commit v3 on v2

--- a/solution.py
+++ b/solution.py
@@ -106,7 +106,12 @@
     gram = jnp.where(row % 2 == column % 2, gram, 0.0)
     adjoint = jnp.concatenate([adjoint_ref[k] for k in range(edges)], axis=0)
     forward = jnp.concatenate([forward_ref[k] for k in range(edges)], axis=0)
-    sens = jnp.sum(forward * dot(gram, adjoint, precision=highest), axis=0, keepdims=True)
+    (gram_a, gram_b), (field_a, field_b) = halves(gram), halves(adjoint)
+    left = [gram_a.astype(F32), gram_b.astype(F32), gram_a.astype(F32)]
+    right = [field_a.astype(F32), field_a.astype(F32), field_b.astype(F32)]
+    left = jnp.concatenate(left, axis=1).astype(BF16)
+    mixed = dot(left, jnp.concatenate(right, axis=0).astype(BF16))
+    sens = jnp.sum(forward * mixed, axis=0, keepdims=True)
     groups = sens.shape[1] // LANES
     sens = jnp.concatenate([sens[:, g * LANES : (g + 1) * LANES] for g in range(groups)], axis=0)
     first, _ = halves(sens)

time: 78.4 us -> 78.3 us (level)
  no operation moved by 1% of the time
where the time goes in v3:
time: 78.3 us; the launch traced here: 78 us
  starting transfers between devices  28.7 us (37%)
  Pallas kernels  20.4 us (26%)
  waiting for transfers between devices  18.2 us (23%)
  blocking collectives  9.89 us (13%)
    all_to_all x1, blocking collectives, update(): lax.all_to_all(ratios, ('tx', 'ty'), split_axis=0, concat_axis=0, tiled=T...  9.89 us
    ppermute x1, waiting for transfers between devices, update(): high_first = lax.ppermute(down_first, 'tx', down)  8.43 us
    all_to_all x1, starting transfers between devices, update(): lax.all_to_all(payload, ('tx', 'ty'), split_axis=0, concat_axis=0, tiled=...  7.43 us
    ppermute x1, starting transfers between devices, update(): low_first = lax.ppermute(up_first, 'tx', up)  7.36 us
    pallas_call x1, Pallas kernels, update(): pl.pallas_call(functools.partial(deposit_kernel, cells_y, slots), out_sha...  6.61 us
    ppermute x1, waiting for transfers between devices, update(): low_first = lax.ppermute(up_first, 'tx', up)  5.34 us
    pallas_call x1, Pallas kernels, update(): partial, ends = call(grid, low_near, high_near, rim, before, after)  4.77 us
    ppermute x1, starting transfers between devices, update(): high_far = lax.ppermute(mains[3], 'tx', down)  3.72 us
  transfers between devices with their start and end apart: 11, of which 4 were waited for; matrix products, arithmetic and copies ran while one was open for 0% of the time, Pallas kernels for 17%

profile of v3, /device:TPU:0, one launch (start us, length us, event | category | flops | bytes accessed | tf_op | source)
XLA Modules:
  0.0 78.0 jit_solution(4816684040574683387)
XLA Ops:
  0.6 2.8 %pack.1.token_ref = bf16[16,56,128]{2,1,0:T(8,128)(2,1)} custom-call(s32[1,16]{1,0:T(1,128)} %counts_ref.1, f32[8]{0:T(128)} %quad_hbm.1, f32[12,24]{1,0:T(8,128)} %bitcast.13, f32[12,2,2048]{2,1,0:T(2,128)} %bitcast.10, f32[12,2,2048]{2,1,0:T(2,128)} %bitcast.11, bf16[16,16,128]{2,1,0:T(8,128)(2,1)} %weights_hbm.1, s32[16,16]{1,0:T(8,128)} %elements_ref.1, ...), custom_call_target="tpu_custom_call" | custom-call | tf_op jit(solution)/shard_map/pack/pallas_call | solution.py:595
  3.4 7.4 %all-to-all-start = ((bf16[16,56,128]{2,1,0:T(8,128)(2,1)}), bf16[16,56,128]{2,1,0:T(8,128)(2,1)S(1)}, u32[]{:S(2)}, u32[]{:S(2)}) async-start(bf16[16,56,128]{2,1,0:T(8,128)(2,1)} %pack.1.token_ref), calls=%async_computation | async-start | bytes 458752 | tf_op jit(solution)/shard_map/all_to_all | solution.py:597
  10.8 1.8 %cast_rims.1 = (bf16[256,128]{1,0:T(8,128)(2,1)S(1)}, bf16[256,128]{1,0:T(8,128)(2,1)S(1)}, bf16[4,240,128]{2,1,0:T(8,128)(2,1)S(1)}, bf16[4,240,128]{2,1,0:T(8,...) custom-call(f32[32,256,128]{2,1,0:T(8,128)} %design_ref.1, ...), custom_call_target="tpu_custom_call" | custom-call | tf_op jit(solution)/shard_map/cast_rims/pallas_call | solution.py:612
  12.7 2.0 %collective-permute-start.2 = (bf16[4,240,128]{2,1,0:T(8,128)(2,1)S(1)}, bf16[4,240,128]{2,1,0:T(8,128)(2,1)S(1)}, u32[]{:S(2)}, u32[]{:S(2)}) collective-permute-start(bf16[4,240,128]{2,1,0:T(8,128)(2,1)S(1)} %get-tuple-element.22), channel_id=1, source_target_pairs={{0,8},{8,16},{16,24},{24,0},{1,9},{9,17},{17,25},{25,1},{2,10},{10... | collective-permute-start | bytes 737288 | tf_op jit(solution)/shard_map/ppermute | solution.py:625
  14.6 1.9 %collective-permute-start.3 = (bf16[4,240,128]{2,1,0:T(8,128)(2,1)S(1)}, bf16[4,240,128]{2,1,0:T(8,128)(2,1)S(1)}, u32[]{:S(2)}, u32[]{:S(2)}) collective-permute-start(bf16[4,240,128]{2,1,0:T(8,128)(2,1)S(1)} %get-tuple-element.23), channel_id=1, source_target_pairs={{8,0},{16,8},{24,16},{0,24},{9,1},{17,9},{25,17},{1,25},{10,2},{18... | collective-permute-start | bytes 737288 | tf_op jit(solution)/shard_map/ppermute | solution.py:626
  16.5 1.9 %collective-permute-start.1 = (bf16[256,128]{1,0:T(8,128)(2,1)S(1)}, bf16[256,128]{1,0:T(8,128)(2,1)S(1)}, u32[]{:S(2)}, u32[]{:S(2)}) collective-permute-start(bf16[256,128]{1,0:T(8,128)(2,1)S(1)} %get-tuple-element.20), channel_id=1, source_target_pairs={{8,0},{16,8},{24,16},{0,24},{9,1},{17,9},{25,17},{1,25},{10,2},{18... | collective-permute-start | bytes 196616 | tf_op jit(solution)/shard_map/ppermute | solution.py:614
  18.5 0.1 collective-permute-start.8
  18.6 3.7 %collective-permute-start.9 = (bf16[4,240,128]{2,1,0:T(8,128)(2,1)S(1)}, bf16[4,240,128]{2,1,0:T(8,128)(2,1)S(1)}, u32[]{:S(2)}, u32[]{:S(2)}) collective-permute-start(bf16[4,240,128]{2,1,0:T(8,128)(2,1)S(1)} %get-tuple-element.32), channel_id=1, source_target_pairs={{8,0},{16,8},{24,16},{0,24},{9,1},{17,9},{25,17},{1,25},{10,2},{18... | collective-permute-start | bytes 737288 | tf_op jit(solution)/shard_map/ppermute | solution.py:628
  22.3 8.4 %collective-permute-done.1.high_ref = bf16[256,128]{1,0:T(8,128)(2,1)S(1)} collective-permute-done((bf16[256,128]{1,0:T(8,128)(2,1)S(1)}, bf16[256,128]{1,0:T(8,128)(2,1)S(1)}, u32[]{:S(2)}, u32[]{:S(2)}) %collective-permute-start.1) | collective-permute-done | bytes 65568 | tf_op jit(solution)/shard_map/ppermute | solution.py:614
  30.7 7.4 %collective-permute-start = (bf16[256,128]{1,0:T(8,128)(2,1)S(1)}, bf16[256,128]{1,0:T(8,128)(2,1)S(1)}, u32[]{:S(2)}, u32[]{:S(2)}) collective-permute-start(bf16[256,128]{1,0:T(8,128)(2,1)S(1)} %get-tuple-element.19.token_ref), channel_id=1, source_target_pairs={{0,8},{8,16},{16,24},{24,0},{1,9},{9,17},{17,25},{25,1},{2,10},{10... | collective-permute-start | bytes 196616 | tf_op jit(solution)/shard_map/ppermute | solution.py:613
  38.1 5.3 %collective-permute-done.low_ref = bf16[256,128]{1,0:T(8,128)(2,1)S(1)} collective-permute-done((bf16[256,128]{1,0:T(8,128)(2,1)S(1)}, bf16[256,128]{1,0:T(8,128)(2,1)S(1)}, u32[]{:S(2)}, u32[]{:S(2)}) %collective-permute-start) | collective-permute-done | bytes 65568 | tf_op jit(solution)/shard_map/ppermute | solution.py:613
  43.5 0.0 all-to-all-done.pay_ref
  43.5 6.6 %deposit.1 = (f32[12288,128]{1,0:T(8,128)S(1)}, f32[32,16,128]{2,1,0:T(8,128)S(1)}, bf16[32,128]{1,0:T(8,128)(2,1)S(1)}, bf16[32,8,256]{2,1,0:T(8,128)(2,1)S(1)}, s32[16,128]{1,0:T(8,128)S(1)}) custom-call(f32[8192,128]{1,0:T(8,128)} %bitcast.9, bf16[256,128]{1,0:T(8,128)(2,1)S(1)} %collective-permute-done.low_ref, ...), custom_call_target="tpu_custom_call" | custom-call | tf_op jit(solution)/shard_map/deposit/pallas_call | solution.py:630
  50.1 1.3 %collective-permute-start.5 = (bf16[32,128]{1,0:T(8,128)(2,1)S(1)}, bf16[32,128]{1,0:T(8,128)(2,1)S(1)}, u32[]{:S(2)}, u32[]{:S(2)}) collective-permute-start(bf16[32,128]{1,0:T(8,128)(2,1)S(1)} %get-tuple-element.26), channel_id=1, source_target_pairs={{0,1},{1,0},{2,3},{3,2},{4,5},{5,4},{6,7},{7,6},{8,9},{9,8},{10,11... | collective-permute-start | bytes 24584 | tf_op jit(solution)/shard_map/ppermute | solution.py:654
  51.4 2.4 %collective-permute-done.5.small_ref = bf16[32,128]{1,0:T(8,128)(2,1)S(1)} collective-permute-done((bf16[32,128]{1,0:T(8,128)(2,1)S(1)}, bf16[32,128]{1,0:T(8,128)(2,1)S(1)}, u32[]{:S(2)}, u32[]{:S(2)}) %collective-permute-start.5) | collective-permute-done | bytes 8224 | tf_op jit(solution)/shard_map/ppermute | solution.py:654
  53.8 1.2 %collective-permute-start.4 = (bf16[32,8,256]{2,1,0:T(8,128)(2,1)S(1)}, bf16[32,8,256]{2,1,0:T(8,128)(2,1)S(1)}, u32[]{:S(2)}, u32[]{:S(2)}) collective-permute-start(bf16[32,8,256]{2,1,0:T(8,128)(2,1)S(1)} %get-tuple-element.24), channel_id=1, source_target_pairs={{0,1},{1,0},{2,3},{3,2},{4,5},{5,4},{6,7},{7,6},{8,9},{9,8},{10,11... | collective-permute-start | bytes 393224 | tf_op jit(solution)/shard_map/ppermute | solution.py:655
  55.0 0.4 edges.1
  55.4 0.0 collective-permute-done.2.low_ref.low_near_ref
  55.4 0.1 collective-permute-start.6
  55.5 0.0 collective-permute-done.3.high_ref.high_near_ref
  55.5 1.7 %collective-permute-start.7 = (bf16[32,8,128]{2,1,0:T(8,128)(2,1)S(1)}, bf16[32,8,128]{2,1,0:T(8,128)(2,1)S(1)}, u32[]{:S(2)}, u32[]{:S(2)}) collective-permute-start(bf16[32,8,128]{2,1,0:T(8,128)(2,1)S(1)} %get-tuple-element.28), channel_id=1, source_target_pairs={{2,0},{4,2},{6,4},{0,6},{3,1},{5,3},{7,5},{1,7},{10,8},{12,10},{14... | collective-permute-start | bytes 196616 | tf_op jit(solution)/shard_map/ppermute | solution.py:669
  57.2 1.9 %collective-permute-done.6.before_ref = bf16[32,8,128]{2,1,0:T(8,128)(2,1)S(1)} collective-permute-done((bf16[32,8,128]{2,1,0:T(8,128)(2,1)S(1)}, bf16[32,8,128]{2,1,0:T(8,128)(2,1)S(1)}, u32[]{:S(2)}, u32[]{:S(2)}) %collective-permute-start.6) | collective-permute-done | bytes 65568 | tf_op jit(solution)/shard_map/ppermute | solution.py:668
  59.1 0.0 collective-permute-done.7.after_ref
  59.1 0.0 collective-permute-done.4.rim_ref
  59.1 4.8 %inner.1 = (f32[8192,128]{1,0:T(8,128)S(1)}, f32[2,256,128]{2,1,0:T(8,128)S(1)}) custom-call(f32[12288,128]{1,0:T(8,128)S(1)} %get-tuple-element.21.grid_ref, bf16[4,240,128]{2,1,0:T(8,128)(2,1)S(1)} %collective-permute-done.2.low_ref.low_near_ref, bf16[4,240,128]{2,1,0:T(8,128)(2,1)S(1)} %collective-permute-done.3.high_ref.high_near_ref, ...), custom_call_target="tpu_custom_call" | custom-call | tf_op jit(solution)/shard_map/inner/pallas_call | solution.py:685
  63.9 0.0 collective-permute-done.8.low_far_ref
  63.9 0.0 collective-permute-done.9.high_far_ref
  63.9 0.0 copy-start
  63.9 0.0 copy-start.1
  64.0 3.1 %finish.1 = (f32[8192,128]{1,0:T(8,128)S(1)}, f32[8192,128]{1,0:T(8,128)}, f32[2,128]{1,0:T(2,128)S(1)}) custom-call(f32[8192,128]{1,0:T(8,128)S(1)} %get-tuple-element.29.inner_ref, s32[16,128]{1,0:T(8,128)S(1)} %get-tuple-element.30.own_ref, f32[12288,128]{1,0:T(8,128)S(1)} %get-tuple-element.21.grid_ref, ...), custom_call_target="tpu_custom_call", output_to_operand_aliasing={{0}: (0, {})} | custom-call | tf_op jit(solution)/shard_map/finish/pallas_call | solution.py:686
  67.0 0.1 all_to_all.11
  67.1 9.9 %all_to_all.16 = f32[16,1,16]{2,1,0:T(1,128)S(1)} all-to-all(f32[16,1,16]{2,1,0:T(1,128)S(1)} %bitcast.12), channel_id=1, replica_groups=mesh['tx'=4,'ty'=4,'gz'=2] {'tx','ty'}, dimensions={0} | all-to-all | bytes 2048 | tf_op jit(solution)/shard_map/all_to_all | solution.py:707
  77.0 0.0 copy-done
  77.0 0.0 copy-done.1
  77.0 1.0 %to_elements.1 = f32[16,128]{1,0:T(8,128)} custom-call(s32[1,16]{1,0:T(1,128)S(1)} %copy-done.1, s32[16,16]{1,0:T(8,128)S(1)} %copy-done, f32[16,16]{1,0:T(8,128)S(1)} %bitcast.8), custom_call_target="tpu_custom_call" | custom-call | tf_op jit(solution)/shard_map/to_elements/pallas_call | solution.py:708
  (1 shorter events, 0.0 us)
Async XLA Ops:
  3.4 40.0 %all-to-all-start = ((bf16[16,56,128]{2,1,0:T(8,128)(2,1)}), bf16[16,56,128]{2,1,0:T(8,128)(2,1)S(1)}, u32[]{:S(2)}, u32[]{:S(2)}) async-start(bf16[16,56,128]{2,1,0:T(8,128)(2,1)} %pack.1.token_ref), calls=%async_computation | async-start | bytes 458752 | tf_op jit(solution)/shard_map/all_to_all | solution.py:597
  12.7 42.7 %collective-permute-start.2 = (bf16[4,240,128]{2,1,0:T(8,128)(2,1)S(1)}, bf16[4,240,128]{2,1,0:T(8,128)(2,1)S(1)}, u32[]{:S(2)}, u32[]{:S(2)}) collective-permute-start(bf16[4,240,128]{2,1,0:T(8,128)(2,1)S(1)} %get-tuple-element.22), channel_id=1, source_target_pairs={{0,8},{8,16},{16,24},{24,0},{1,9},{9,17},{17,25},{25,1},{2,10},{10... | collective-permute-start | bytes 737288 | tf_op jit(solution)/shard_map/ppermute | solution.py:625
  14.6 40.8 %collective-permute-start.3 = (bf16[4,240,128]{2,1,0:T(8,128)(2,1)S(1)}, bf16[4,240,128]{2,1,0:T(8,128)(2,1)S(1)}, u32[]{:S(2)}, u32[]{:S(2)}) collective-permute-start(bf16[4,240,128]{2,1,0:T(8,128)(2,1)S(1)} %get-tuple-element.23), channel_id=1, source_target_pairs={{8,0},{16,8},{24,16},{0,24},{9,1},{17,9},{25,17},{1,25},{10,2},{18... | collective-permute-start | bytes 737288 | tf_op jit(solution)/shard_map/ppermute | solution.py:626
  16.5 14.2 %collective-permute-start.1 = (bf16[256,128]{1,0:T(8,128)(2,1)S(1)}, bf16[256,128]{1,0:T(8,128)(2,1)S(1)}, u32[]{:S(2)}, u32[]{:S(2)}) collective-permute-start(bf16[256,128]{1,0:T(8,128)(2,1)S(1)} %get-tuple-element.20), channel_id=1, source_target_pairs={{8,0},{16,8},{24,16},{0,24},{9,1},{17,9},{25,17},{1,25},{10,2},{18... | collective-permute-start | bytes 196616 | tf_op jit(solution)/shard_map/ppermute | solution.py:614
  18.5 45.4 %collective-permute-start.8 = (bf16[4,240,128]{2,1,0:T(8,128)(2,1)S(1)}, bf16[4,240,128]{2,1,0:T(8,128)(2,1)S(1)}, u32[]{:S(2)}, u32[]{:S(2)}) collective-permute-start(bf16[4,240,128]{2,1,0:T(8,128)(2,1)S(1)} %get-tuple-element.31), channel_id=1, source_target_pairs={{0,8},{8,16},{16,24},{24,0},{1,9},{9,17},{17,25},{25,1},{2,10},{10... | collective-permute-start | bytes 737288 | tf_op jit(solution)/shard_map/ppermute | solution.py:627
  18.6 45.3 %collective-permute-start.9 = (bf16[4,240,128]{2,1,0:T(8,128)(2,1)S(1)}, bf16[4,240,128]{2,1,0:T(8,128)(2,1)S(1)}, u32[]{:S(2)}, u32[]{:S(2)}) collective-permute-start(bf16[4,240,128]{2,1,0:T(8,128)(2,1)S(1)} %get-tuple-element.32), channel_id=1, source_target_pairs={{8,0},{16,8},{24,16},{0,24},{9,1},{17,9},{25,17},{1,25},{10,2},{18... | collective-permute-start | bytes 737288 | tf_op jit(solution)/shard_map/ppermute | solution.py:628
  30.7 12.7 %collective-permute-start = (bf16[256,128]{1,0:T(8,128)(2,1)S(1)}, bf16[256,128]{1,0:T(8,128)(2,1)S(1)}, u32[]{:S(2)}, u32[]{:S(2)}) collective-permute-start(bf16[256,128]{1,0:T(8,128)(2,1)S(1)} %get-tuple-element.19.token_ref), channel_id=1, source_target_pairs={{0,8},{8,16},{16,24},{24,0},{1,9},{9,17},{17,25},{25,1},{2,10},{10... | collective-permute-start | bytes 196616 | tf_op jit(solution)/shard_map/ppermute | solution.py:613
  50.1 3.7 %collective-permute-start.5 = (bf16[32,128]{1,0:T(8,128)(2,1)S(1)}, bf16[32,128]{1,0:T(8,128)(2,1)S(1)}, u32[]{:S(2)}, u32[]{:S(2)}) collective-permute-start(bf16[32,128]{1,0:T(8,128)(2,1)S(1)} %get-tuple-element.26), channel_id=1, source_target_pairs={{0,1},{1,0},{2,3},{3,2},{4,5},{5,4},{6,7},{7,6},{8,9},{9,8},{10,11... | collective-permute-start | bytes 24584 | tf_op jit(solution)/shard_map/ppermute | solution.py:654
  53.8 5.3 %collective-permute-start.4 = (bf16[32,8,256]{2,1,0:T(8,128)(2,1)S(1)}, bf16[32,8,256]{2,1,0:T(8,128)(2,1)S(1)}, u32[]{:S(2)}, u32[]{:S(2)}) collective-permute-start(bf16[32,8,256]{2,1,0:T(8,128)(2,1)S(1)} %get-tuple-element.24), channel_id=1, source_target_pairs={{0,1},{1,0},{2,3},{3,2},{4,5},{5,4},{6,7},{7,6},{8,9},{9,8},{10,11... | collective-permute-start | bytes 393224 | tf_op jit(solution)/shard_map/ppermute | solution.py:655
  55.4 3.7 %collective-permute-start.6 = (bf16[32,8,128]{2,1,0:T(8,128)(2,1)S(1)}, bf16[32,8,128]{2,1,0:T(8,128)(2,1)S(1)}, u32[]{:S(2)}, u32[]{:S(2)}) collective-permute-start(bf16[32,8,128]{2,1,0:T(8,128)(2,1)S(1)} %get-tuple-element.27), channel_id=1, source_target_pairs={{0,2},{2,4},{4,6},{6,0},{1,3},{3,5},{5,7},{7,1},{8,10},{10,12},{12... | collective-permute-start | bytes 196616 | tf_op jit(solution)/shard_map/ppermute | solution.py:668
  55.5 3.7 %collective-permute-start.7 = (bf16[32,8,128]{2,1,0:T(8,128)(2,1)S(1)}, bf16[32,8,128]{2,1,0:T(8,128)(2,1)S(1)}, u32[]{:S(2)}, u32[]{:S(2)}) collective-permute-start(bf16[32,8,128]{2,1,0:T(8,128)(2,1)S(1)} %get-tuple-element.28), channel_id=1, source_target_pairs={{2,0},{4,2},{6,4},{0,6},{3,1},{5,3},{7,5},{1,7},{10,8},{12,10},{14... | collective-permute-start | bytes 196616 | tf_op jit(solution)/shard_map/ppermute | solution.py:669
  63.9 13.1 %copy-start = (s32[16,16]{1,0:T(8,128)S(1)}, s32[16,16]{1,0:T(8,128)}, u32[]{:S(2)}) copy-start(s32[16,16]{1,0:T(8,128)} %elements_ref.1) | copy-start | bytes 3076
  63.9 13.1 %copy-start.1 = (s32[1,16]{1,0:T(1,128)S(1)}, s32[1,16]{1,0:T(1,128)}, u32[]{:S(2)}) copy-start(s32[1,16]{1,0:T(1,128)} %counts_ref.1) | copy-start | bytes 196
